TPU v7x, 128 devices: a whole 4x4x4 slice. The times are simulated.
128 devices in a mesh: rep: 2 (over core), dp: 64 (over x, y, z).
Axes of the slice: x: 4, y: 4, z: 4, core: 2. Of those that a mesh axis runs over, the one named last changes fastest.
Arguments:
- x: bfloat16 [128, 2048, 1024], P(('rep', 'dp')), parts along dimension 0
- dy: bfloat16 [128, 2048, 1024], P(('rep', 'dp')), parts along dimension 0
- w_gate: bfloat16 [2, 1024, 3328], replicated
- w_up: bfloat16 [2, 1024, 3328], replicated
- w_down: bfloat16 [2, 3328, 1024], replicated
- m_w_gate: float32 [2, 1024, 3328], replicated
- m_w_up: float32 [2, 1024, 3328], replicated
- m_w_down: float32 [2, 3328, 1024], replicated
- v_w_gate: float32 [2, 1024, 3328], replicated
- v_w_up: float32 [2, 1024, 3328], replicated
- v_w_down: float32 [2, 3328, 1024], replicated
Outputs:
- output 1: bfloat16 [4, 1024, 3328], P('rep'), parts along dimension 0
- output 2: bfloat16 [4, 1024, 3328], P('rep'), parts along dimension 0
- output 3: bfloat16 [4, 3328, 1024], P('rep'), parts along dimension 0
- output 4: float32 [4, 1024, 3328], P('rep'), parts along dimension 0
- output 5: float32 [4, 1024, 3328], P('rep'), parts along dimension 0
- output 6: float32 [4, 3328, 1024], P('rep'), parts along dimension 0
- output 7: float32 [4, 1024, 3328], P('rep'), parts along dimension 0
- output 8: float32 [4, 1024, 3328], P('rep'), parts along dimension 0
- output 9: float32 [4, 3328, 1024], P('rep'), parts along dimension 0
There are 2 independent parts. A program takes and returns all parts, laid end to end along the dimension named above; an argument that names none is the same for every part.
All inputs are finite; a program needn't handle non-finite values.
Results may differ from a plain program's by a relative error of at most 0.022.
Values are sent between devices in bfloat16 or wider.
A program may use at most 1.5 GiB of HBM per device.

v0:
```python
import jax
import jax.numpy as jnp
from jax import lax
from jax.sharding import PartitionSpec as P

NAMES = ("w_gate", "w_up", "w_down")


def matmul(a, w):
    return jnp.dot(a, w, preferred_element_type=jnp.float32).astype(jnp.bfloat16)


def normed(h):
    wide = h.astype(jnp.float32)
    scale = lax.rsqrt(jnp.mean(wide**2, -1, keepdims=True) + 1e-6)
    return (wide * scale).astype(jnp.bfloat16)


def layer(h, w):
    a = normed(h)
    gate = jnp.dot(a, w["w_gate"], preferred_element_type=jnp.float32)
    up = jnp.dot(a, w["w_up"], preferred_element_type=jnp.float32)
    return h + matmul((jax.nn.silu(gate) * up).astype(jnp.bfloat16), w["w_down"])


def adamw(w, m, v, g):
    m = 0.9 * m + 0.1 * g
    v = 0.95 * v + 0.05 * g * g
    step = m * lax.rsqrt(v + 1e-8) + 0.1 * w
    return (w - 0.02 * step).astype(jnp.bfloat16), m, v


def solution(mesh):
    def step(x, dy, *arrays):
        weights, m, v = (arrays[i : i + 3] for i in (0, 3, 6))
        layers = weights[0].shape[0]
        h, kept = x[0], []
        for number in range(layers):
            kept.append(h)
            h = layer(h, {name: w[number] for name, w in zip(NAMES, weights, strict=True)})
        by_h, summed = dy[0], [None] * layers
        for number in reversed(range(layers)):
            _, back = jax.vjp(lambda w, h: layer(h, w), {name: w[number] for name, w in zip(NAMES, weights, strict=True)}, kept[number])
            by_w, by_h = back(by_h)
            summed[number] = [lax.psum(by_w[name], "dp") for name in NAMES]
        gradients = [jnp.stack([summed[number][i] for number in range(layers)]).astype(jnp.float32) for i in range(3)]
        new = [adamw(w.astype(jnp.float32), m, v, g) for w, m, v, g in zip(weights, m, v, gradients, strict=True)]
        return tuple(one[which] for which in range(3) for one in new)

    return jax.shard_map(
        step,
        mesh=mesh,
        in_specs=(P(("rep", "dp"), None, None),) * 2 + (P(None, None, None),) * 9,
        out_specs=(P("rep", None, None),) * 9,
        check_vma=False,
    )
```

profile of v0, /device:TPU:1, one launch (start us, length us, event | category | flops | bytes accessed | tf_op | source)
XLA Modules:
  0.0 939.6 jit_solution(5406566047478606606)
XLA Ops:
  7.2 0.0 all-reduce.3.cloned.1.call-start
  7.2 6.6 copy.20
  13.8 3.1 fusion.30
  16.8 0.0 copy-start.5
  16.9 6.5 copy.21
  23.3 21.0 %convolution_convert_fusion.1 = bf16[2048,3328]{1,0:T(8,128)(2,1)} fusion(bf16[2,3328,1024]{2,1,0:T(8,128)(2,1)} %param.15, bf16[1,2048,1024]{2,1,0:T(8,128)(2,1)} %param.12), kind=kOutput, calls=%fused_computation.50 | convolution fusion | flops 13965459456 | bytes 24641536 | tf_op jit(solution)/shard_map/transpose(jvp())/dot_general | solution.py:10
  44.3 0.0 copy-start.2
  44.3 22.3 %fusion.56 = f32[2048,3328]{1,0:T(8,128)} fusion(bf16[2,1024,3328]{2,1,0:T(8,128)(2,1)} %param.13, bf16[1,2048,1024]{2,1,0:T(8,128)(2,1)} %param.11, f32[2048]{0:T(1024)S(1)} %add_rsqrt_fusion), kind=kOutput, calls=%fused_computation.90 | convolution fusion | flops 13964935168 | bytes 38281216 | tf_op jit(solution)/shard_map/dot_general | solution.py:21
  66.6 0.0 copy-done.5
  66.6 0.0 copy-done.2
  66.6 29.0 %multiply_convert_fusion.1 = (bf16[2048,3328]{1,0:T(8,128)(2,1)}, f32[2048,3328]{1,0:T(8,128)}) fusion(f32[2048,3328]{1,0:T(8,128)} %fusion.56, bf16[2,1024,3328]{2,1,0:T(8,128)(2,1)} %param.14, bf16[1,2048,1024]{2,1,0:T(8,128)(2,1)S(1)} %copy-done.2, f32[2048]{0:T(1024)S(1)} %add_rsqrt_fusion), kind=kOutput, calls=%fused_computation.44 | convolution fusion | flops 14005829632 | bytes 79175680 | tf_op jit(solution)/shard_map/dot_general | solution.py:22
  95.6 22.1 %fusion.34 = (f32[2048]{0:T(1024)S(1)}, bf16[2048,1024]{0,1:T(8,128)(2,1)}) fusion(bf16[2048,3328]{1,0:T(8,128)(2,1)} %get-tuple-element.24, bf16[2,3328,1024]{2,1,0:T(8,128)(2,1)} %param.15, bf16[1,2048,1024]{1,2,0:T(8,128)(2,1)} %copy.20), kind=kOutput, calls=%fused_computation.67 | convolution fusion | flops 13969127424 | bytes 28844032 | tf_op jit(solution)/shard_map/dot_general | solution.py:10
  117.7 0.0 copy-start.3
  117.7 23.8 %fusion.43 = f32[2048,3328]{1,0:T(8,128)} fusion(bf16[2,1024,3328]{2,1,0:T(8,128)(2,1)} %param.14, bf16[2048,1024]{0,1:T(8,128)(2,1)} %get-tuple-element.27, f32[2048]{0:T(1024)S(1)} %fusion.92), kind=kOutput, calls=%fused_computation.77 | convolution fusion | flops 13964935168 | bytes 38281216 | tf_op jit(solution)/shard_map/jvp()/dot_general | solution.py:22
  141.5 0.0 copy-done.3
  141.5 40.0 %fusion.14 = (bf16[2048,3328]{1,0:T(8,128)(2,1)}, f32[2048,3328]{1,0:T(8,128)}) fusion(f32[2048,3328]{1,0:T(8,128)} %fusion.43, bf16[2048,3328]{1,0:T(8,128)(2,1)} %convolution_convert_fusion.1, bf16[2,1024,3328]{2,1,0:T(8,128)(2,1)} %param.13, bf16[2048,1024]{0,1:T(8,128)(2,1)} %get-tuple-element.27, f32[2048]{0:T(1024)S(1)} %fusion.92), kind=kOutput, calls=%fused_computation.32 | convolution fusion | flops 14046724096 | bytes 92807168 | tf_op jit(solution)/shard_map/jvp()/dot_general | solution.py:21
  181.5 0.0 copy-start.1
  181.5 22.9 %fusion.27 = bf16[2048,1024]{0,1:T(8,128)(2,1)} fusion(bf16[2048,3328]{1,0:T(8,128)(2,1)} %convolution_convert_fusion.1, bf16[2,1024,3328]{2,1,0:T(8,128)(2,1)} %param.14, f32[2048,3328]{1,0:T(8,128)} %get-tuple-element.29), kind=kOutput, calls=%fused_computation.48 | convolution fusion | flops 13999538176 | bytes 51904512 | tf_op jit(solution)/shard_map/transpose(jvp())/dot_general | solution.py:22
  204.4 0.0 copy-done.1
  204.4 24.3 %fusion.64 = bf16[1,1024,3328]{2,1,0:T(8,128)(2,1)} fusion(bf16[2048,3328]{1,0:T(8,128)(2,1)} %convolution_convert_fusion.1, bf16[2048,1024]{0,1:T(8,128)(2,1)S(1)} %copy-done.1, f32[2048]{0:T(1024)S(1)} %fusion.92, f32[2048,3328]{1,0:T(8,128)} %get-tuple-element.29), kind=kOutput, calls=%fused_computation.98 | convolution fusion | flops 14009237504 | bytes 51912704 | tf_op jit(solution)/shard_map/transpose(jvp())/dot_general | solution.py:22
  228.7 26.9 %fusion.65 = bf16[1,3328,1024]{2,1,0:T(8,128)(2,1)} fusion(f32[2048,3328]{1,0:T(8,128)} %fusion.43, bf16[1,2048,1024]{2,1,0:T(8,128)(2,1)} %param.12, f32[2048,3328]{1,0:T(8,128)} %get-tuple-element.29), kind=kOutput, calls=%fused_computation.99 | convolution fusion | flops 14002946048 | bytes 65536000 | tf_op jit(solution)/shard_map/transpose(jvp())/dot_general | solution.py:10
  255.6 21.6 %fusion.61 = bf16[1,1024,3328]{2,1,0:T(8,128)(2,1)} fusion(bf16[2048,3328]{1,0:T(8,128)(2,1)} %get-tuple-element.28, bf16[2048,1024]{0,1:T(8,128)(2,1)} %get-tuple-element.27, f32[2048]{0:T(1024)S(1)} %fusion.92), kind=kOutput, calls=%fused_computation.95 | convolution fusion | flops 13964935168 | bytes 24649728 | tf_op jit(solution)/shard_map/transpose(jvp())/dot_general | solution.py:21
  277.2 0.0 copy-start.4
  277.2 22.8 %fusion.36 = (f32[2048]{0:T(1024)S(1)}, bf16[2048,1024]{0,1:T(8,128)(2,1)}) fusion(bf16[2048,1024]{0,1:T(8,128)(2,1)} %get-tuple-element.27, bf16[2048,1024]{0,1:T(8,128)(2,1)} %fusion.27, bf16[2048,3328]{1,0:T(8,128)(2,1)} %get-tuple-element.28, bf16[2,1024,3328]{2,1,0:T(8,128)(2,1)} %param.13), kind=kOutput, calls=%fused_computation.69 | convolution fusion | flops 13969127424 | bytes 33038336 | tf_op jit(solution)/shard_map/transpose(jvp())/dot_general | solution.py:21
  300.1 0.0 copy-done.4
  300.1 7.6 fusion.77
  307.7 21.2 %convolution_convert_fusion = bf16[2048,3328]{1,0:T(8,128)(2,1)} fusion(bf16[2048,1024]{0,1:T(8,128)(2,1)} %fusion.77, bf16[2,3328,1024]{2,1,0:T(8,128)(2,1)} %param.15), kind=kOutput, calls=%fused_computation.49 | convolution fusion | flops 13965459456 | bytes 24641536 | tf_op jit(solution)/shard_map/transpose(jvp())/dot_general | solution.py:10
  328.8 0.0 copy-start
  328.8 0.0 copy-start.6
  328.8 20.9 %fusion.62 = bf16[1,3328,1024]{2,1,0:T(8,128)(2,1)} fusion(bf16[2048,3328]{1,0:T(8,128)(2,1)} %get-tuple-element.24, bf16[2048,1024]{0,1:T(8,128)(2,1)} %fusion.77), kind=kOutput, calls=%fused_computation.96 | convolution fusion | flops 13962051584 | bytes 24641536 | tf_op jit(solution)/shard_map/transpose(jvp())/dot_general | solution.py:10
  349.8 0.0 copy-done
  349.8 0.0 copy-done.6
  349.8 24.4 %fusion.63 = bf16[1,1024,3328]{2,1,0:T(8,128)(2,1)} fusion(bf16[2048,3328]{1,0:T(8,128)(2,1)} %convolution_convert_fusion, f32[2048,3328]{1,0:T(8,128)} %fusion.56, bf16[1,2048,1024]{1,2,0:T(8,128)(2,1)S(1)} %copy-done, f32[2048]{0:T(1024)S(1)} %copy-done.6), kind=kOutput, calls=%fused_computation.97 | convolution fusion | flops 14009237504 | bytes 51912704 | tf_op jit(solution)/shard_map/transpose(jvp())/dot_general | solution.py:22
  374.2 31.0 %fusion.66 = bf16[1,1024,3328]{2,1,0:T(8,128)(2,1)} fusion(f32[2048,3328]{1,0:T(8,128)} %fusion.56, f32[2048,3328]{1,0:T(8,128)} %get-tuple-element.25, bf16[2048,3328]{1,0:T(8,128)(2,1)} %convolution_convert_fusion, bf16[1,2048,1024]{1,2,0:T(8,128)(2,1)} %copy.20, f32[2048]{0:T(1024)S(1)} %copy-done.6), kind=kOutput, calls=%fused_computation.100 | convolution fusion | flops 14043316224 | bytes 79175680 | tf_op jit(solution)/shard_map/transpose(jvp())/dot_general | solution.py:21
  405.2 0.0 all-reduce.3.cloned.1.call-update
  405.2 382.2 %all-reduce.3.cloned.1.call-done = (bf16[1,1024,3328]{2,1,0:T(8,128)(2,1)}, bf16[1,1024,3328]{2,1,0:T(8,128)(2,1)}, bf16[1,1024,3328]{2,1,0:T(8,128)(2,1)}, bf16...) async-done(((bf16[1,1024,3328]{2,1,0:T(8,128)(2,1)}, bf16[1,1024,3328]{2,1,0:T(8,128)(2,1)}, ...) | async-done | bytes 40894480 | tf_op jit(solution)/shard_map/psum | solution.py:45
  787.4 51.6 %fusion.11 = (bf16[2,3328,1024]{2,1,0:T(8,128)(2,1)}, f32[2,3328,1024]{2,1,0:T(8,128)}, f32[2,3328,1024]{2,1,0:T(8,128)}) fusion(bf16[2,3328,1024]{2,1,0:T(8,128)(2,1)} %param.15, bf16[1,3328,1024]{2,1,0:T(8,128)(2,1)} %get-tuple-element.13, bf16[1,3328,1024]{2,1,0:T(8,128)(2,1)} %get-tuple-element.14, f32[2,3328,1024]{2,1,0:T(8,128)} %param.21, ...), kind=kLoop, calls=%fused_computation.29 | loop fusion | flops 129499136 | bytes 149946368 | tf_op jit(solution)/shard_map/convert_element_type | solution.py:30
  839.0 93.3 %fusion.2 = (bf16[2,1024,3328]{2,1,0:T(8,128)(2,1)}, f32[2,1024,3328]{2,1,0:T(8,128)}, f32[2,1024,3328]{2,1,0:T(8,128)}, bf16[2,1024,3328]{2,1,0:T(8,128)(2,1)},...) fusion(bf16[2,1024,3328]{2,1,0:T(8,128)(2,1)} %param.13, bf16[1,1024,3328]{2,1,0:T(8,128)(2,1)} %get-tuple-element.9, ...), kind=kLoop, calls=%fused_computation.20 | loop fusion | flops 258998272 | bytes 299892736 | tf_op jit(solution)/shard_map/convert_element_type | solution.py:30
  (3 shorter events, 0.0 us)
Async XLA Ops:
  7.2 780.2 %all-reduce.3.cloned.1.call-start = ((), (), s32[]{:S(2)}) async-start(), calls=%async_computation | async-start | bytes 81788928 | tf_op jit(solution)/shard_map/psum | solution.py:45
  16.8 49.8 %copy-start.5 = (f32[2048]{0:T(1024)}, f32[2048]{0:T(1024)S(1)}, u32[]{:S(2)}) copy-start(f32[2048]{0:T(1024)S(1)} %add_rsqrt_fusion) | copy-start | bytes 24580
  44.3 22.3 %copy-start.2 = (bf16[1,2048,1024]{2,1,0:T(8,128)(2,1)S(1)}, bf16[1,2048,1024]{2,1,0:T(8,128)(2,1)}, u32[]{:S(2)}) copy-start(bf16[1,2048,1024]{2,1,0:T(8,128)(2,1)} %param.11) | copy-start | bytes 12582916
  117.7 23.8 %copy-start.3 = (f32[2048]{0:T(1024)}, f32[2048]{0:T(1024)S(1)}, u32[]{:S(2)}) copy-start(f32[2048]{0:T(1024)S(1)} %get-tuple-element.26) | copy-start | bytes 24580
  181.5 22.9 %copy-start.1 = (bf16[2048,1024]{0,1:T(8,128)(2,1)S(1)}, bf16[2048,1024]{0,1:T(8,128)(2,1)}, u32[]{:S(2)}) copy-start(bf16[2048,1024]{0,1:T(8,128)(2,1)} %get-tuple-element.27) | copy-start | bytes 12582916
  277.2 22.8 %copy-start.4 = (f32[2048]{0:T(1024)S(1)}, f32[2048]{0:T(1024)}, u32[]{:S(2)}) copy-start(f32[2048]{0:T(1024)} %copy-done.3) | copy-start | bytes 24580
  328.8 20.9 %copy-start = (bf16[1,2048,1024]{1,2,0:T(8,128)(2,1)S(1)}, bf16[1,2048,1024]{1,2,0:T(8,128)(2,1)}, u32[]{:S(2)}) copy-start(bf16[1,2048,1024]{1,2,0:T(8,128)(2,1)} %copy.20) | copy-start | bytes 12582916
  328.8 20.9 %copy-start.6 = (f32[2048]{0:T(1024)S(1)}, f32[2048]{0:T(1024)}, u32[]{:S(2)}) copy-start(f32[2048]{0:T(1024)} %copy-done.5) | copy-start | bytes 24580
Sparse Core Ops, SparseCore 0:
  405.3 382.0 all-reduce.2
where the time goes:
time: 951 us; the launch traced here: 940 us
  waiting for transfers between devices  382 us (40%)
  matrix products  374 us (39%)
  other arithmetic  156 us (16%)
  between operations  14.6 us (2%)
  local copies, waits for them, and re-layouts  13.1 us (1%)
    psum x1, waiting for transfers between devices, step(): summed[number] = [lax.psum(by_w[name], 'dp') for name in NAMES]  382 us
    convert_element_type x2, other arithmetic, adamw(): return ((w - 0.02 * step).astype(jnp.bfloat16), m, v)  145 us
    dot_general x5, matrix products, layer(): gate = jnp.dot(a, w['w_gate'], preferred_element_type=jnp.float32)  138 us
    dot_general x5, matrix products, layer(): up = jnp.dot(a, w['w_up'], preferred_element_type=jnp.float32)  124 us
    dot_general x5, matrix products, matmul(): jnp.dot(a, w, preferred_element_type=jnp.float32).astype(jnp.bfloat16)  112 us
  transfers between devices with their start and end apart: 1, of which 1 were waited for; matrix products, arithmetic and copies ran while one was open for 0% of the time, Pallas kernels for 0%

commit v1 on v0

v1 whole, which is shorter than its diff:
```python
import functools

import jax
import jax.numpy as jnp
from jax import lax
from jax.experimental import pallas as pl
from jax.experimental.pallas import tpu as pltpu
from jax.sharding import PartitionSpec as P

T, D, FF, SL = 2048, 1024, 3328, 256
NS = FF // SL
TB = 512
F32, BF = jnp.float32, jnp.bfloat16
MESH = pl.DeviceIdType.MESH
VMEM_LIMIT = 66_900_000
COMM = True

OFF = (0, 2, 5, 7, 9, 11, 13, 15, 17, 19, 21, 24, 26)
NR = 12
SLOTS = 3


def dot(a, b):
    return lax.dot_general(a, b, (((1,), (0,)), ((), ())), preferred_element_type=F32)


def dot_nt(a, b):
    return lax.dot_general(a, b, (((1,), (1,)), ((), ())), preferred_element_type=F32)


def normed(h):
    wide = h.astype(F32)
    scale = lax.rsqrt(jnp.mean(wide * wide, -1, keepdims=True) + 1e-6)
    return (wide * scale).astype(BF)


def forward_kernel(x_ref, dy_ref, wg_ref, wu_ref, wd_ref, gate_ref, up_ref, h1_ref, a1_ref, a0t_ref, a1t_ref, dyt_ref, a0, acc, stage, sem):
    j = pl.program_id(0)

    @pl.when(j == 0)
    def _():
        def one(b, c):
            rows = pl.ds(pl.multiple_of(b * TB, TB), TB)
            a = normed(x_ref[rows, :])
            a0[rows, :] = a
            acc[rows, :] = jnp.zeros((TB, D), F32)
            return c

        lax.fori_loop(0, T // TB, one, 0)

    def transposed(src, dst):
        def one(b, c):
            rows = pl.ds(pl.multiple_of(b * TB, TB), TB)
            stage[:, rows] = src[rows, :].T
            return c

        lax.fori_loop(0, T // TB, one, 0)
        copy = pltpu.make_async_copy(stage, dst, sem)
        copy.start()
        copy.wait()

    @pl.when(j == 1)
    def _():
        transposed(a0, a0t_ref)

    @pl.when(j == 2)
    def _():
        transposed(dy_ref, dyt_ref)

    def one(b, c):
        rows = pl.ds(pl.multiple_of(b * TB, TB), TB)
        a = a0[rows, :]
        gate = dot(a, wg_ref[0])
        up = dot(a, wu_ref[0])
        gate_ref[0, rows, :] = gate
        up_ref[0, rows, :] = up
        hid = (gate * jax.nn.sigmoid(gate) * up).astype(BF)
        acc[rows, :] += dot(hid, wd_ref[0])
        return c

    lax.fori_loop(0, T // TB, one, 0)

    @pl.when(j == NS - 1)
    def _():
        def one(b, c):
            rows = pl.ds(pl.multiple_of(b * TB, TB), TB)
            h1 = (x_ref[rows, :].astype(F32) + acc[rows, :].astype(BF).astype(F32)).astype(BF)
            h1_ref[rows, :] = h1
            a1_ref[rows, :] = normed(h1)
            return c

        lax.fori_loop(0, T // TB, one, 0)
        transposed(a1_ref, a1t_ref)


def forward(x, dy, wg, wu, wd):
    whole = pl.BlockSpec((T, D), lambda j: (0, 0))
    wide = pl.BlockSpec((1, T, SL), lambda j: (j, 0, 0))
    anyspec = pl.BlockSpec(memory_space=pl.ANY)
    return pl.pallas_call(
        forward_kernel,
        name="forward",
        grid=(NS,),
        in_specs=[
            whole,
            whole,
            pl.BlockSpec((1, D, SL), lambda j: (0, 0, j)),
            pl.BlockSpec((1, D, SL), lambda j: (0, 0, j)),
            pl.BlockSpec((1, SL, D), lambda j: (0, j, 0)),
        ],
        out_specs=[wide, wide, whole, whole, anyspec, anyspec, anyspec],
        out_shape=[
            jax.ShapeDtypeStruct((NS, T, SL), F32),
            jax.ShapeDtypeStruct((NS, T, SL), F32),
            jax.ShapeDtypeStruct((T, D), BF),
            jax.ShapeDtypeStruct((T, D), BF),
            jax.ShapeDtypeStruct((D, T), BF),
            jax.ShapeDtypeStruct((D, T), BF),
            jax.ShapeDtypeStruct((D, T), BF),
        ],
        scratch_shapes=[pltpu.VMEM((T, D), BF), pltpu.VMEM((T, D), F32), pltpu.VMEM((D, T), BF), pltpu.SemaphoreType.DMA],
        compiler_params=pltpu.CompilerParams(vmem_limit_bytes=VMEM_LIMIT),
        cost_estimate=pl.CostEstimate(flops=6 * T * D * FF, bytes_accessed=100_000_000, transcendentals=T * FF),
    )(x, dy, wg, wu, wd)


def backward_kernel(
    a1_ref, dy_ref, a1t_ref, dyt_ref, h1_ref, a0t_ref, gate_ref, up_ref, wg_ref, wu_ref, wd_ref,
    g1_ref, g0_ref,
    act, by, actt, byt, acc, hid, dgt, dup, wgb, wub, wdb,
    grad, s1, s2, sa0, ra0, sb0, rb0, sa1, ra1, sb1, rb1, sa2, ra2, sb2, rb2, cb, g0b,
    wsem, asem, lsem, send, recv,
):
    me = lax.axis_index("dp")
    xyz = (lax.div(me, 16), lax.rem(lax.div(me, 4), 4), lax.rem(me, 4))
    stride = (16, 4, 1)
    axes = [[(m + k) % 3 for k in range(3)] for m in range(3)]
    plus = [me + (lax.rem(xyz[d] + 1, 4) - xyz[d]) * stride[d] for d in range(3)]
    minus = [me + (lax.rem(xyz[d] + 3, 4) - xyz[d]) * stride[d] for d in range(3)]
    digit = [[xyz[d] for d in axes[m]] for m in range(3)]
    to = [[(plus[d], minus[d]) for d in axes[m]] for m in range(3)]

    def turn(c, k):
        return lax.rem(c + k, 4)

    def block(c, size):
        return pl.ds(pl.multiple_of(c * size, size), size)

    if COMM:
        barrier = pltpu.get_barrier_semaphore()
        for d in range(3):
            for n in (plus[d], minus[d]):
                pl.semaphore_signal(barrier, inc=1, device_id={"dp": n}, device_id_type=MESH)
        pl.semaphore_wait(barrier, 6)

    HALF = (pl.ds(0, 128), pl.ds(128, 128))
    sas, ras, sbs, rbs = (sa0, sa1, sa2), (ra0, ra1, ra2), (sb0, sb1, sb2), (rb0, rb1, rb2)
    sizes = (256, 64, 16)

    def parts(r, s, m, k):
        two, three = lax.rem(s, 2), lax.rem(s, 3)
        if r < 6:
            ph = r // 2
            if r % 2 == 0:
                return sas[ph].at[two, m, k], ras[ph].at[two, m, k]
            slot = three if ph == 0 else two
            return sbs[ph].at[slot, m, k], rbs[ph].at[slot, m, k]
        eight = lax.rem(s, 8)
        ph = 2 - (r - 6) // 2
        c = digit[m][ph]
        size = sizes[ph]
        if ph == 0:
            if r % 2 == 0:
                return cb.at[eight, m], g1_ref.at[m, s, block(c, size)]
            ref = g1_ref.at[m, s, block(turn(c, 3 if k == 0 else 1), size), HALF[k]]
            return ref, ref
        base = block(digit[m][1] * 4 + c, size) if ph == 2 else block(c, size)
        if r % 2 == 0:
            return cb.at[eight, m, base], cb.at[eight, m, base]
        c = turn(c, 3 if k == 0 else 1)
        base = block(digit[m][1] * 4 + c, size) if ph == 2 else block(c, size)
        return cb.at[eight, m, base, HALF[k]], cb.at[eight, m, base, HALF[k]]

    def copies(r, s):
        slot = lax.rem(s, SLOTS)
        ph = r // 2 if r < 6 else 2 - (r - 6) // 2
        for m in range(3):
            for k in range(2):
                src, dst = parts(r, s, m, k)
                yield pltpu.make_async_remote_copy(
                    src_ref=src,
                    dst_ref=dst,
                    send_sem=send.at[r, slot, m, k],
                    recv_sem=recv.at[r, slot, m, k],
                    device_id={"dp": to[m][ph][k]},
                    device_id_type=MESH,
                )

    def finish(r, s):
        for copy in copies(r, s):
            copy.wait()

    def own_copy(s, m):
        return pltpu.make_async_copy(
            cb.at[lax.rem(s, 8), m], g1_ref.at[m, s, block(digit[m][0], 256)], lsem.at[lax.rem(s, SLOTS), m]
        )

    def prepare(r, s):
        two, three, eight = lax.rem(s, 2), lax.rem(s, 3), lax.rem(s, 8)
        if r > 0:
            finish(r - 1, s)
        if r <= 6:
            ph = r // 2
            size = sizes[min(ph, 2)]
            total = (grad, s1, s2)[min(ph, 2)]
            for m in range(3):
                if r % 2 == 0 and r > 0:
                    before = (grad, s1, s2)[ph - 1]
                    slot = three if ph == 1 else two
                    mine = before[three, m, block(digit[m][ph - 1], sizes[ph - 1]), :]
                    mine = mine + rbs[ph - 1][slot, m, 0].astype(F32) + rbs[ph - 1][slot, m, 1].astype(F32)
                    if r < 6:
                        total[three, m] = mine
                    else:
                        done = mine.astype(BF)

                        @pl.when(s < NS)
                        def _():
                            cb[eight, m, block(digit[m][1] * 4 + digit[m][2], 16), :] = done

                        @pl.when(s >= NS)
                        def _():
                            g0b[m, s - NS] = done

                if r < 6 and r % 2 == 0:
                    far = block(turn(digit[m][ph], 2), size)
                    for k in range(2):
                        sas[ph][two, m, k] = total[three, m, far, HALF[k]].astype(BF)
                if r < 6 and r % 2 == 1:
                    slot = three if ph == 0 else two
                    for k in range(2):
                        near = block(turn(digit[m][ph], 1 if k == 0 else 3), size)
                        add, keep = HALF[k], HALF[1 - k]
                        sbs[ph][slot, m, k, :, add] = (total[three, m, near, add] + ras[ph][two, m, k].astype(F32)).astype(BF)
                        sbs[ph][slot, m, k, :, keep] = total[three, m, near, keep].astype(BF)
        if r == NR:
            for m in range(3):
                own_copy(s, m).wait()

    def start(r, s):
        for copy in copies(r, s):
            copy.start()
        if r == 10:
            for m in range(3):
                own_copy(s, m).start()

    def service(i, half):
        if not COMM:
            return
        todo = []
        for r in range(NR + 1):
            if OFF[r] % 2 == (1 - half):
                back = (OFF[r] + 1 - half) // 2
                todo.append((r, back))
        for r, back in todo:
            s = i - back

            @pl.when((s >= 0) & (s < (2 * NS if r <= 6 else NS)))
            def _():
                prepare(r, s)

        for r, back in todo:
            if r == NR:
                continue
            s = i - back

            @pl.when((s >= 0) & (s < (2 * NS if r < 6 else NS)))
            def _():
                start(r, s)

    def weights(i):
        slot = lax.rem(i, 2)
        first = i < NS
        j = lax.rem(i, NS)
        columns = block(j, SL)
        down = pltpu.make_async_copy(wd_ref.at[jnp.where(first, 1, 0), columns, :], wdb.at[slot], wsem.at[slot, 0])
        one = [
            pltpu.make_async_copy(wg_ref.at[1, :, columns], wgb.at[slot], wsem.at[slot, 1]),
            pltpu.make_async_copy(wu_ref.at[1, :, columns], wub.at[slot], wsem.at[slot, 2]),
        ]
        zero = [
            pltpu.make_async_copy(gate_ref.at[j], acc.at[2 * slot], wsem.at[slot, 1]),
            pltpu.make_async_copy(up_ref.at[j], acc.at[2 * slot + 1], wsem.at[slot, 2]),
        ]
        return down, one, zero

    loads = [
        pltpu.make_async_copy(a1_ref, act, asem.at[0]),
        pltpu.make_async_copy(dy_ref, by, asem.at[1]),
        pltpu.make_async_copy(a1t_ref, actt, asem.at[2]),
        pltpu.make_async_copy(dyt_ref, byt, asem.at[3]),
    ]
    down, one, _ = weights(0)
    for copy in [down, *one, *loads]:
        copy.start()

    def clear(b, c):
        rows = block(b, TB)
        for n in range(4):
            acc[n, rows, :] = jnp.zeros((TB, SL), F32)
        return c

    lax.fori_loop(0, T // TB, clear, 0)
    loads[0].wait()
    loads[1].wait()
    h1_load = pltpu.make_async_copy(h1_ref, act, asem.at[0])
    a0t_load = pltpu.make_async_copy(a0t_ref, actt, asem.at[2])

    def second_layer(i):
        slot = lax.rem(i, 2)
        down, one, _ = weights(i)
        for copy in [down, *one]:
            copy.wait()

        @pl.when(i + 1 < NS)
        def _():
            down, one, _ = weights(i + 1)
            for copy in [down, *one]:
                copy.start()

        def tokens(b, c):
            rows = block(b, TB)
            a = act[rows, :]
            gate = dot(a, wgb[slot])
            up = dot(a, wub[slot])
            by_hid = dot_nt(by[rows, :], wdb[slot]).astype(BF).astype(F32)
            sig = jax.nn.sigmoid(gate)
            silu = gate * sig
            hid[rows, :] = (silu * up).astype(BF)
            by_up = (by_hid * silu).astype(BF)
            by_gate = (by_hid * up * (sig * (1.0 + gate * (1.0 - sig)))).astype(BF)
            dup[rows, :] = by_up
            dgt[rows, :] = by_gate
            for n in range(4):
                acc[n, rows, :] += dot_nt(by_gate, wgb[slot, pl.ds(n * SL, SL), :]) + dot_nt(by_up, wub[slot, pl.ds(n * SL, SL), :])
            return c

        lax.fori_loop(0, T // TB, tokens, 0)

    def between(i):
        h1_load.wait()
        a0t_load.start()
        down, _, zero = weights(i)
        down.start()

        def tokens(b, c):
            rows = pl.ds(pl.multiple_of(b * 256, 256), 256)
            wide = act[rows, :].astype(F32)
            scale = lax.rsqrt(jnp.mean(wide * wide, -1, keepdims=True) + 1e-6)
            da = jnp.concatenate([acc[n, rows, :] for n in range(4)], axis=1).astype(BF).astype(F32)
            t = jnp.mean(da * wide, -1, keepdims=True)
            dwide = (da * scale - wide * (scale * scale * scale * t)).astype(BF)
            by_h = (by[rows, :].astype(F32) + dwide.astype(F32)).astype(BF)
            by[rows, :] = by_h
            byt[:, rows] = by_h.T
            return c

        lax.fori_loop(0, T // 256, tokens, 0)
        for copy in zero:
            copy.start()
        a0t_load.wait()

    def first_layer(i):
        slot = lax.rem(i, 2)

        @pl.when(i == NS)
        def _():
            between(i)

        down, _, zero = weights(i)
        for copy in [down, *zero]:
            copy.wait()

        @pl.when(i + 1 < 2 * NS)
        def _():
            down, _, zero = weights(i + 1)
            for copy in [down, *zero]:
                copy.start()

        def tokens(b, c):
            rows = block(b, TB)
            gate = acc[2 * slot, rows, :]
            up = acc[2 * slot + 1, rows, :]
            by_hid = dot_nt(by[rows, :], wdb[slot]).astype(BF).astype(F32)
            sig = jax.nn.sigmoid(gate)
            silu = gate * sig
            hid[rows, :] = (silu * up).astype(BF)
            dup[rows, :] = (by_hid * silu).astype(BF)
            dgt[rows, :] = (by_hid * up * (sig * (1.0 + gate * (1.0 - sig)))).astype(BF)
            return c

        lax.fori_loop(0, T // TB, tokens, 0)

    def iteration(i, c):
        @pl.when(i < NS)
        def _():
            second_layer(i)

        @pl.when(i == 0)
        def _():
            loads[2].wait()
            loads[3].wait()

        @pl.when(i == NS - 1)
        def _():
            h1_load.start()

        @pl.when((i >= NS) & (i < 2 * NS))
        def _():
            first_layer(i)

        service(i, 0)

        @pl.when(i < 2 * NS)
        def _():
            three = lax.rem(i, 3)
            for m, (left, right) in enumerate(((actt, dgt), (actt, dup), (byt, hid))):
                grad[three, m] = dot(left[...], right[...])

        service(i, 1)
        return c

    count = max(2 * NS + 7, NS + 14) if COMM else 2 * NS
    lax.fori_loop(0, count, iteration, 0)
    out = pltpu.make_async_copy(g0b, g0_ref, asem.at[0])
    out.start()
    out.wait()


def backward(a1, dy, a1t, dyt, h1, a0t, gate, up, wg, wu, wd):
    anyspec = pl.BlockSpec(memory_space=pl.ANY)
    V = pltpu.VMEM
    DMA = pltpu.SemaphoreType.DMA
    return pl.pallas_call(
        backward_kernel,
        name="backward",
        in_specs=[anyspec] * 11,
        out_specs=[anyspec] * 2,
        out_shape=[jax.ShapeDtypeStruct((3, NS, D, SL), BF), jax.ShapeDtypeStruct((3, NS, 16, SL), BF)],
        scratch_shapes=[
            V((T, D), BF), V((T, D), BF), V((D, T), BF), V((D, T), BF), V((4, T, SL), F32),
            V((T, SL), BF), V((T, SL), BF), V((T, SL), BF),
            V((2, D, SL), BF), V((2, D, SL), BF), V((2, SL, D), BF),
            V((3, 3, 1024, SL), F32), V((3, 3, 256, SL), F32), V((3, 3, 64, SL), F32),
            V((2, 3, 2, 256, 128), BF), V((2, 3, 2, 256, 128), BF), V((3, 3, 2, 256, SL), BF), V((3, 3, 2, 256, SL), BF),
            V((2, 3, 2, 64, 128), BF), V((2, 3, 2, 64, 128), BF), V((2, 3, 2, 64, SL), BF), V((2, 3, 2, 64, SL), BF),
            V((2, 3, 2, 16, 128), BF), V((2, 3, 2, 16, 128), BF), V((2, 3, 2, 16, SL), BF), V((2, 3, 2, 16, SL), BF),
            V((8, 3, 256, SL), BF), V((3, NS, 16, SL), BF),
            DMA((2, 3)), DMA((4,)), DMA((SLOTS, 3)), DMA((NR, SLOTS, 3, 2)), DMA((NR, SLOTS, 3, 2)),
        ],
        compiler_params=pltpu.CompilerParams(vmem_limit_bytes=VMEM_LIMIT, collective_id=0 if COMM else None, has_side_effects=True),
        cost_estimate=pl.CostEstimate(flops=24 * T * D * FF, bytes_accessed=150_000_000, transcendentals=2 * T * FF),
    )(a1, dy, a1t, dyt, h1, a0t, gate, up, wg, wu, wd)


def adam_kernel(gathered, *refs):
    ins, rest = refs[:12], refs[12:]
    if gathered:
        rest = rest[9:]
    outs, rest = rest[:9], rest[9:]
    for m in range(3):
        w_ref, m_ref, v_ref, g_ref = ins[m], ins[3 + m], ins[6 + m], ins[9 + m]
        w_out, m_out, v_out = outs[m], outs[3 + m], outs[6 + m]

        def take(at, g):
            g = g.astype(F32)
            w = w_ref[at].astype(F32)
            mean = 0.9 * m_ref[at] + 0.1 * g
            var = 0.95 * v_ref[at] + 0.05 * g * g
            w_out[at] = (w - 0.02 * (mean * lax.rsqrt(var + 1e-8) + 0.1 * w)).astype(BF)
            m_out[at] = mean
            v_out[at] = var

        if gathered:
            whole = rest[0]
            for n in range(64):
                digits = (n // 16, n // 4 % 4, n % 4)
                xyz = [digits[(d - m) % 3] for d in range(3)]
                whole[n * 16 : n * 16 + 16, :] = g_ref[xyz[0] * 16 + xyz[1] * 4 + xyz[2], 0, 0]
            look = lambda rows: whole[rows, :]
        else:
            look = lambda rows: g_ref[0, 0, rows, :]

        if m < 2:

            def one(b, c):
                rows = pl.ds(pl.multiple_of(b * 64, 64), 64)
                take((0, rows, slice(None)), look(rows))
                return c

            lax.fori_loop(0, D // 64, one, 0)
        else:

            def one(b, c):
                rows = pl.ds(pl.multiple_of(b * 128, 128), 128)
                take((0, slice(None), rows), look(rows).T)
                return c

            lax.fori_loop(0, D // 128, one, 0)


def adam(layer, weights, means, variances, gradients, so_far=None):
    wide = pl.BlockSpec((1, D, SL), lambda j: (layer, 0, j))
    tall = pl.BlockSpec((1, SL, D), lambda j: (layer, j, 0))
    mine = [wide, wide, tall]
    gathered = so_far is not None
    if gathered:
        grads = [pl.BlockSpec((64, 1, 1, 16, SL), functools.partial(lambda m, j: (0, m, j, 0, 0), m)) for m in range(3)]
    else:
        grads = [pl.BlockSpec((1, 1, D, SL), functools.partial(lambda m, j: (m, j, 0, 0), m)) for m in range(3)]
    shapes = [jax.ShapeDtypeStruct(a.shape, a.dtype) for a in (*weights, *means, *variances)]
    return pl.pallas_call(
        functools.partial(adam_kernel, gathered),
        name=f"adam{layer}",
        grid=(NS,),
        in_specs=mine * 3 + grads + ([pl.BlockSpec(memory_space=pl.ANY)] * 9 if gathered else []),
        out_specs=mine * 3,
        out_shape=shapes,
        input_output_aliases={12 + k: k for k in range(9)} if gathered else {},
        scratch_shapes=[pltpu.VMEM((D, SL), BF)] if gathered else [],
        compiler_params=pltpu.CompilerParams(vmem_limit_bytes=VMEM_LIMIT),
        cost_estimate=pl.CostEstimate(flops=10**10, bytes_accessed=66 * D * FF, transcendentals=3 * D * FF),
    )(*weights, *means, *variances, *[gradients] * 3, *(so_far or ()))


def solution(mesh):
    def step(x, dy, *arrays):
        x, dy = x[0], dy[0]
        weights, means, variances = (arrays[k : k + 3] for k in (0, 3, 6))
        gate, up, h1, a1, a0t, a1t, dyt = forward(x, dy, *weights)
        g1, g0 = backward(a1, dy, a1t, dyt, h1, a0t, gate, up, *weights)
        g0 = lax.all_gather(g0, "dp", axis=0)
        new = adam(1, weights, means, variances, g1)
        return tuple(adam(0, weights, means, variances, g0, new))

    return jax.shard_map(
        step,
        mesh=mesh,
        in_specs=(P(("rep", "dp"), None, None),) * 2 + (P(None, None, None),) * 9,
        out_specs=(P("rep", None, None),) * 9,
        check_vma=False,
    )
```

time: 951 us -> 630 us (0.66); the launches traced: 940 us -> 630 us
  Pallas kernels: 0 us -> 576 us
  matrix products: 374 us -> 0 us
  waiting for transfers between devices: 382 us -> 40 us
  other arithmetic: 156 us -> 0 us
  local copies, waits for them, and re-layouts: 13.1 us -> 0 us
    pallas_call x0 -> x4, Pallas kernels: none -> 576 us  [the longest x1 342 us: backward(): pl.pallas_call(backward_kernel, name='backward', in_specs=[anyspec] * 11,...]
    psum x1 -> x0, waiting for transfers between devices: 382 us -> none  [step(): summed[number] = [lax.psum(by_w[name], 'dp') for name in NAMES]]
    dot_general x15 -> x0, matrix products: 374 us -> none  [the longest x5 138 us: layer(): gate = jnp.dot(a, w['w_gate'], preferred_element_type=jnp.float32)]
    convert_element_type x2 -> x0, other arithmetic: 145 us -> none  [adamw(): return ((w - 0.02 * step).astype(jnp.bfloat16), m, v)]
    all_gather x0 -> x1, waiting for transfers between devices: none -> 40 us  [step(): g0 = lax.all_gather(g0, 'dp', axis=0)]
    unnamed x16 -> x0, local copies, waits for them, and re-layouts: 13.1 us -> none
  transfers between devices with their start and end apart: 1 -> 1, of which waited for: 1 -> 1; matrix products, arithmetic and copies ran while one was open for 0% -> 0% of each run, Pallas kernels for 0% -> 13%
where the time goes in v1:
time: 630 us
  Pallas kernels  576 us (91%)
  waiting for transfers between devices  40 us (6%)
  between operations  14.1 us (2%)
    pallas_call x1, Pallas kernels, backward(): pl.pallas_call(backward_kernel, name='backward', in_specs=[anyspec] * 11,...  342 us
    pallas_call x2, Pallas kernels, adam(): pl.pallas_call(functools.partial(adam_kernel, gathered), name=f'adam{laye...  159 us
    pallas_call x1, Pallas kernels, forward(): pl.pallas_call(forward_kernel, name='forward', grid=(NS,), in_specs=[whol...  75 us
    all_gather x1, waiting for transfers between devices, step(): g0 = lax.all_gather(g0, 'dp', axis=0)  40 us
  transfers between devices with their start and end apart: 1, of which 1 were waited for; matrix products, arithmetic and copies ran while one was open for 0% of the time, Pallas kernels for 13%

profile of v1, /device:TPU:1, one launch (start us, length us, event | category | flops | bytes accessed | tf_op | source)
XLA Modules:
  0.0 629.9 jit_solution(3476493077880411792)
XLA Ops:
  7.2 0.0 all-gather.3.cloned.1.call-start
  7.2 75.0 %forward.1 = (f32[13,2048,256]{2,1,0:T(8,128)}, f32[13,2048,256]{2,1,0:T(8,128)}, bf16[2048,1024]{1,0:T(8,128)(2,1)}, bf16[2048,1024]{1,0:T(8,128)(2,1)}, bf16[1...) custom-call(bf16[2048,1024]{1,0:T(8,128)(2,1)} %bitcast.6, ...), custom_call_target="tpu_custom_call" | custom-call | flops 41875931136 | bytes 100000000 | tf_op jit(solution)/shard_map/forward/pallas_call | solution.py:100
  82.2 341.8 %backward.1 = (bf16[3,13,1024,256]{3,2,1,0:T(8,128)(2,1)}, bf16[3,13,16,256]{3,2,1,0:T(8,128)(2,1)}) custom-call(bf16[2048,1024]{1,0:T(8,128)(2,1)} %get-tuple-element.27.a1_ref, bf16[2048,1024]{1,0:T(8,128)(2,1)} %bitcast.8, bf16[1024,2048]{1,0:T(8,128)(2,1)} %get-tuple-element.28.a1t_ref, bf16[1024,2048]{1,0:T(8,128)(2,1)} %get-tuple-element.29.dyt_ref, ...), custom_call_target="tpu_custom_call" | custom-call | flops 167503724544 | bytes 150000000 | tf_op jit(solution)/shard_map/backward/pallas_call | solution.py:444
  424.0 0.0 all-gather.3.cloned.1.call-update
  424.0 79.1 %adam1.1 = (bf16[2,1024,3328]{2,1,0:T(8,128)(2,1)}, bf16[2,1024,3328]{2,1,0:T(8,128)(2,1)}, bf16[2,3328,1024]{2,1,0:T(8,128)(2,1)}, f32[2,1024,3328]{2,1,0:T(8,1...) custom-call(bf16[2,1024,3328]{2,1,0:T(8,128)(2,1)} %refs_0_.3, ...), custom_call_target="tpu_custom_call" | custom-call | flops 10000000000 | bytes 224919552 | tf_op jit(solution)/shard_map/adam1/pallas_call | solution.py:522
  503.2 40.0 %all-gather.3.cloned.1.call-done = bf16[192,13,16,256]{3,2,1,0:T(8,128)(2,1)} async-done(((bf16[3,13,16,256]{3,2,1,0:T(8,128)(2,1)}), bf16[192,13,16,256]{3,2,1,0:T(8,128)(2,1)}) %all-gather.3.cloned.1.call-update) | async-done | bytes 20447248 | tf_op jit(solution)/shard_map/all_gather | solution.py:542
  543.2 79.9 %adam0.1 = (bf16[2,1024,3328]{2,1,0:T(8,128)(2,1)}, bf16[2,1024,3328]{2,1,0:T(8,128)(2,1)}, bf16[2,3328,1024]{2,1,0:T(8,128)(2,1)}, f32[2,1024,3328]{2,1,0:T(8,1...) custom-call(bf16[2,1024,3328]{2,1,0:T(8,128)(2,1)} %refs_0_.3, ...), custom_call_target="tpu_custom_call", output_to_operand_aliasing={{0}: (12, {}), {1}: (13, {}), {2}: (14, {}), {3}: (15, {}),... | custom-call | flops 10000000000 | bytes 224919552 | tf_op jit(solution)/shard_map/adam0/pallas_call | solution.py:522
Async XLA Ops:
  7.2 536.0 %all-gather.3.cloned.1.call-start = ((), (), s32[]{:S(2)}) async-start(), calls=%async_computation | async-start | bytes 20766720 | tf_op jit(solution)/shard_map/all_gather | solution.py:542
Sparse Core Ops, SparseCore 0:
  424.2 118.9 all-gather.2

commit v2 on v1

v2 whole, which is shorter than its diff:
```python
import functools

import jax
import jax.numpy as jnp
from jax import lax
from jax.experimental import pallas as pl
from jax.experimental.pallas import tpu as pltpu
from jax.sharding import PartitionSpec as P

T, D, FF, SL = 2048, 1024, 3328, 256
NS = FF // SL
TB = 512
H = 256
FB, FH = 2048, 512
F32, BF = jnp.float32, jnp.bfloat16
MESH = pl.DeviceIdType.MESH
VMEM_LIMIT = 66_900_000

STEPS1, MID, STEPS0 = 4, 4, 2
START0 = STEPS1 * NS + MID
OFF = (0, 2, 5, 7, 9, 11, 13, 15, 17, 20, 23, 29, 32)
NR = 12
SLOTS, SEMS, GRADS, CB = 4, 4, 4, 8
Q = 3
CUT = 2


def dot(a, b):
    return lax.dot_general(a, b, (((1,), (0,)), ((), ())), preferred_element_type=F32)


def dot_nt(a, b):
    return lax.dot_general(a, b, (((1,), (1,)), ((), ())), preferred_element_type=F32)


def normed(h):
    wide = h.astype(F32)
    scale = lax.rsqrt(jnp.mean(wide * wide, -1, keepdims=True) + 1e-6)
    return (wide * scale).astype(BF)


def pipelined(count, parts, *stages):
    size = T // count // parts

    def one(b, c):
        rows = [pl.ds(pl.multiple_of(b * (size * parts) + p * size, size), size) for p in range(parts)]
        values = [()] * parts
        for step in range(parts + len(stages) - 1):
            for k, stage in enumerate(stages):
                p = step - k
                if 0 <= p < parts:
                    out = stage(rows[p], *values[p])
                    values[p] = out if isinstance(out, tuple) else (out,)
        return c

    lax.fori_loop(0, count, one, 0)


def forward_kernel(x_ref, dy_ref, wg_ref, wu_ref, wd_ref, gate_ref, up_ref, h1_ref, a1_ref, a0t_ref, a1t_ref, dyt_ref, a0, acc, stage, sem):
    j = pl.program_id(0)

    @pl.when(j == 0)
    def _():
        def one(b, c):
            rows = pl.ds(pl.multiple_of(b * TB, TB), TB)
            a = normed(x_ref[rows, :])
            a0[rows, :] = a
            acc[rows, :] = jnp.zeros((TB, D), F32)
            return c

        lax.fori_loop(0, T // TB, one, 0)

    def transposed(src, dst):
        def one(b, c):
            rows = pl.ds(pl.multiple_of(b * TB, TB), TB)
            stage[:, rows] = src[rows, :].T
            return c

        lax.fori_loop(0, T // TB, one, 0)
        copy = pltpu.make_async_copy(stage, dst, sem)
        copy.start()
        copy.wait()

    @pl.when(j == 1)
    def _():
        transposed(a0, a0t_ref)

    @pl.when(j == 2)
    def _():
        transposed(dy_ref, dyt_ref)

    def gate_up(rows):
        a = a0[rows, :]
        return dot(a, wg_ref[0]), dot(a, wu_ref[0])

    def hidden(rows, gate, up):
        gate_ref[0, rows, :] = gate
        up_ref[0, rows, :] = up
        return (gate * jax.nn.sigmoid(gate) * up).astype(BF)

    def down(rows, hid):
        acc[rows, :] += dot(hid, wd_ref[0])

    pipelined(T // FB, FB // FH, gate_up, hidden, down)

    @pl.when(j == NS - 1)
    def _():
        def one(b, c):
            rows = pl.ds(pl.multiple_of(b * TB, TB), TB)
            h1 = (x_ref[rows, :].astype(F32) + acc[rows, :].astype(BF).astype(F32)).astype(BF)
            h1_ref[rows, :] = h1
            a1_ref[rows, :] = normed(h1)
            return c

        lax.fori_loop(0, T // TB, one, 0)
        transposed(a1_ref, a1t_ref)


def forward(x, dy, wg, wu, wd):
    whole = pl.BlockSpec((T, D), lambda j: (0, 0))
    wide = pl.BlockSpec((1, T, SL), lambda j: (j, 0, 0))
    anyspec = pl.BlockSpec(memory_space=pl.ANY)
    return pl.pallas_call(
        forward_kernel,
        name="forward",
        grid=(NS,),
        in_specs=[
            whole,
            whole,
            pl.BlockSpec((1, D, SL), lambda j: (0, 0, j)),
            pl.BlockSpec((1, D, SL), lambda j: (0, 0, j)),
            pl.BlockSpec((1, SL, D), lambda j: (0, j, 0)),
        ],
        out_specs=[wide, wide, whole, whole, anyspec, anyspec, anyspec],
        out_shape=[
            jax.ShapeDtypeStruct((NS, T, SL), F32),
            jax.ShapeDtypeStruct((NS, T, SL), F32),
            jax.ShapeDtypeStruct((T, D), BF),
            jax.ShapeDtypeStruct((T, D), BF),
            jax.ShapeDtypeStruct((D, T), BF),
            jax.ShapeDtypeStruct((D, T), BF),
            jax.ShapeDtypeStruct((D, T), BF),
        ],
        scratch_shapes=[pltpu.VMEM((T, D), BF), pltpu.VMEM((T, D), F32), pltpu.VMEM((D, T), BF), pltpu.SemaphoreType.DMA],
        compiler_params=pltpu.CompilerParams(vmem_limit_bytes=VMEM_LIMIT),
        cost_estimate=pl.CostEstimate(flops=6 * T * D * FF, bytes_accessed=100_000_000, transcendentals=T * FF),
    )(x, dy, wg, wu, wd)


def backward_kernel(
    a1_ref, dy_ref, a1t_ref, dyt_ref, h1_ref, a0t_ref, gate_ref, up_ref, wg_ref, wu_ref, wd_ref,
    g1_ref, g0_ref,
    act, by, actt, byt, acc, hid, dgt, dup, wgb, wub, wdb,
    grad, s1, s2, sa0, ra0, sb0, rb0, sa1, ra1, sb1, rb1, sa2, ra2, sb2, rb2, cb, g0b,
    wsem, asem, lsem, send, recv,
):
    me = lax.axis_index("dp")
    xyz = (lax.div(me, 16), lax.rem(lax.div(me, 4), 4), lax.rem(me, 4))
    stride = (16, 4, 1)
    axes = [[(m + k) % 3 for k in range(3)] for m in range(3)]
    plus = [me + (lax.rem(xyz[d] + 1, 4) - xyz[d]) * stride[d] for d in range(3)]
    minus = [me + (lax.rem(xyz[d] + 3, 4) - xyz[d]) * stride[d] for d in range(3)]
    digit = [[xyz[d] for d in axes[m]] for m in range(3)]
    to = [[(plus[d], minus[d]) for d in axes[m]] for m in range(3)]

    def turn(c, k):
        return lax.rem(c + k, 4)

    def block(c, size):
        return pl.ds(pl.multiple_of(c * size, size), size)

    barrier = pltpu.get_barrier_semaphore()
    for d in range(3):
        for n in (plus[d], minus[d]):
            pl.semaphore_signal(barrier, inc=1, device_id={"dp": n}, device_id_type=MESH)
    pl.semaphore_wait(barrier, 6)

    HALF = (pl.ds(0, 128), pl.ds(128, 128))
    sas, ras, sbs, rbs = (sa0, sa1, sa2), (ra0, ra1, ra2), (sb0, sb1, sb2), (rb0, rb1, rb2)
    sizes = (256, 64, 16)

    def parts(r, s, m, k):
        slot = lax.rem(s, SLOTS)
        if r < 6:
            ph = r // 2
            send_buf, recv_buf = (sas[ph], ras[ph]) if r % 2 == 0 else (sbs[ph], rbs[ph])
            return send_buf.at[slot, m, k], recv_buf.at[slot, m, k]
        cbm = cb.at[lax.rem(s, CB), m]
        ph = 2 - (r - 6) // 2
        c = digit[m][ph]
        if r % 2 == 1:
            c = turn(c, 3 if k == 0 else 1)
        rows = block(digit[m][1] * 4 + c, 16) if ph == 2 else block(c, sizes[ph])
        if ph == 0:
            out = g1_ref.at[m, s, rows]
            return (cbm, out) if r % 2 == 0 else (out.at[:, HALF[k]], out.at[:, HALF[k]])
        at = cbm.at[rows] if r % 2 == 0 else cbm.at[rows, HALF[k]]
        return at, at

    def copies(r, s):
        slot = lax.rem(s, SEMS)
        ph = r // 2 if r < 6 else 2 - (r - 6) // 2
        for m in range(3):
            for k in range(2):
                src, dst = parts(r, s, m, k)
                yield pltpu.make_async_remote_copy(
                    src_ref=src,
                    dst_ref=dst,
                    send_sem=send.at[r, slot, m, k],
                    recv_sem=recv.at[r, slot, m, k],
                    device_id={"dp": to[m][ph][k]},
                    device_id_type=MESH,
                )

    def own_copy(s, m):
        return pltpu.make_async_copy(
            cb.at[lax.rem(s, CB), m], g1_ref.at[m, s, block(digit[m][0], 256)], lsem.at[lax.rem(s, SEMS), m]
        )

    def total(ph, s):
        return grad.at[lax.rem(s, GRADS)] if ph == 0 else (s1, s2)[ph - 1].at[lax.rem(s, SLOTS)]

    def mine(ph, s, m):
        slot = lax.rem(s, SLOTS)
        rows = block(digit[m][ph], sizes[ph])
        return total(ph, s)[m, rows, :] + rbs[ph][slot, m, 0].astype(F32) + rbs[ph][slot, m, 1].astype(F32)

    def prepare(r, s):
        slot = lax.rem(s, SLOTS)
        if r > 0:
            for copy in copies(r - 1, s):
                copy.wait()
        for m in range(3):
            ph = r // 2
            if r in (2, 4):
                total(ph, s)[m] = mine(ph - 1, s, m)
            if r in (0, 2, 4):
                far = block(turn(digit[m][ph], 2), sizes[ph])
                for k in range(2):
                    sas[ph][slot, m, k] = total(ph, s)[m, far, HALF[k]].astype(BF)
            if r in (1, 3, 5):
                for k in range(2):
                    near = block(turn(digit[m][ph], 1 if k == 0 else 3), sizes[ph])
                    add, keep = HALF[k], HALF[1 - k]
                    sbs[ph][slot, m, k, :, add] = (total(ph, s)[m, near, add] + ras[ph][slot, m, k].astype(F32)).astype(BF)
                    sbs[ph][slot, m, k, :, keep] = total(ph, s)[m, near, keep].astype(BF)
            if r == 6:
                done = mine(2, s, m).astype(BF)

                @pl.when(s < NS + Q)
                def _():
                    cb[lax.rem(s, CB), m, block(digit[m][1] * 4 + digit[m][2], 16), :] = done

                @pl.when(s >= NS + Q)
                def _():
                    g0b[m, s - NS - Q] = done

            if r == NR:
                own_copy(s, m).wait()

    def start(r, s):
        for copy in copies(r, s):
            copy.start()
        if r == 10:
            for m in range(3):
                own_copy(s, m).start()

    def service(h):
        q1, r1 = lax.div(h, STEPS1), lax.rem(h, STEPS1)
        q0, r0 = lax.div(h, STEPS0), lax.rem(h, STEPS0)
        todo = []
        for r in (2, 3, 4, 5, 0, 1, 6, 7, 8, 9, 10, 11, 12):
            from1, from0 = STEPS1 - 1 + OFF[r], START0 + STEPS0 - 1 + OFF[r]
            one = (r1 == from1 % STEPS1) & (h >= from1) & (h < from1 + STEPS1 * NS)

            def zero(count):
                return (r0 == from0 % STEPS0) & (h >= from0) & (h < from0 + STEPS0 * count)

            s = jnp.where(h >= from0, NS + q0 - from0 // STEPS0, q1 - from1 // STEPS1)
            prepared = one | zero(NS if r <= 6 else Q)
            todo.append((r, s, prepared, one | zero(Q) if r == 6 else prepared))
        for r, s, prepared, _ in todo:
            pl.when(prepared)(functools.partial(prepare, r, s))
        for r, s, _, sent in todo:
            if r < NR:
                pl.when(sent)(functools.partial(start, r, s))

    def weights(i):
        slot = lax.rem(i, 2)
        first = i < NS
        j = lax.rem(i, NS)
        columns = block(j, SL)
        down = pltpu.make_async_copy(wd_ref.at[jnp.where(first, 1, 0), columns, :], wdb.at[slot], wsem.at[slot, 0])
        one = [
            pltpu.make_async_copy(wg_ref.at[1, :, columns], wgb.at[slot], wsem.at[slot, 1]),
            pltpu.make_async_copy(wu_ref.at[1, :, columns], wub.at[slot], wsem.at[slot, 2]),
        ]
        zero = [
            pltpu.make_async_copy(gate_ref.at[j], acc.at[2 * slot], wsem.at[slot, 1]),
            pltpu.make_async_copy(up_ref.at[j], acc.at[2 * slot + 1], wsem.at[slot, 2]),
        ]
        return down, one, zero

    loads = [
        pltpu.make_async_copy(a1_ref, act, asem.at[0]),
        pltpu.make_async_copy(dy_ref, by, asem.at[1]),
        pltpu.make_async_copy(a1t_ref, actt, asem.at[2]),
        pltpu.make_async_copy(dyt_ref, byt, asem.at[3]),
    ]
    down, one, _ = weights(0)
    for copy in [down, *one, *loads]:
        copy.start()

    def clear(b, c):
        rows = block(b, TB)
        for n in range(4):
            acc[n, rows, :] = jnp.zeros((TB, SL), F32)
        return c

    lax.fori_loop(0, T // TB, clear, 0)
    loads[0].wait()
    loads[1].wait()
    h1_load = pltpu.make_async_copy(h1_ref, act, asem.at[0])
    a0t_load = pltpu.make_async_copy(a0t_ref, actt, asem.at[2])

    def second_layer(i, part):
        slot = lax.rem(i, 2)

        @pl.when(part == 0)
        def _():
            down, one, _ = weights(i)
            for copy in [down, *one]:
                copy.wait()

            @pl.when(i + 1 < NS)
            def _():
                down, one, _ = weights(i + 1)
                for copy in [down, *one]:
                    copy.start()

        def products(rows):
            a = act[rows, :]
            return dot(a, wgb[slot]), dot(a, wub[slot]), dot_nt(by[rows, :], wdb[slot])

        def elements(rows, gate, up, by_hid):
            by_hid = by_hid.astype(BF).astype(F32)
            sig = jax.nn.sigmoid(gate)
            silu = gate * sig
            hid[rows, :] = (silu * up).astype(BF)
            by_up = (by_hid * silu).astype(BF)
            by_gate = (by_hid * up * (sig * (1.0 + gate * (1.0 - sig)))).astype(BF)
            dup[rows, :] = by_up
            dgt[rows, :] = by_gate
            return by_gate, by_up

        def back(rows, by_gate, by_up):
            for n in range(4):
                acc[n, rows, :] += dot_nt(by_gate, wgb[slot, pl.ds(n * SL, SL), :]) + dot_nt(by_up, wub[slot, pl.ds(n * SL, SL), :])

        half = T // 2
        count = half // H
        rows = [pl.ds(pl.multiple_of(part * half + p * H, H), H) for p in range(count)]
        d, e = [None] * count, [None] * count
        for p in range(count + 2):
            if p < count:
                d[p] = products(rows[p])
            if 0 <= p - 1 < count:
                e[p - 1] = elements(rows[p - 1], *d[p - 1])
            if 0 <= p - 2 < count:
                back(rows[p - 2], *e[p - 2])

    def between(part):
        @pl.when(part == 0)
        def _():
            h1_load.wait()
            a0t_load.start()
            weights(NS)[0].start()

        quarter = T // MID

        def tokens(b, c):
            rows = pl.ds(pl.multiple_of(part * quarter + b * H, H), H)
            wide = act[rows, :].astype(F32)
            scale = lax.rsqrt(jnp.mean(wide * wide, -1, keepdims=True) + 1e-6)
            da = jnp.concatenate([acc[n, rows, :] for n in range(4)], axis=1).astype(BF).astype(F32)
            t = jnp.mean(da * wide, -1, keepdims=True)
            dwide = (da * scale - wide * (scale * scale * scale * t)).astype(BF)
            by_h = (by[rows, :].astype(F32) + dwide.astype(F32)).astype(BF)
            by[rows, :] = by_h
            byt[:, rows] = by_h.T
            return c

        lax.fori_loop(0, quarter // H, tokens, 0)

        @pl.when(part == MID - 1)
        def _():
            for copy in weights(NS)[2]:
                copy.start()
            a0t_load.wait()

    def first_layer(i):
        slot = lax.rem(i, 2)
        down, _, zero = weights(i)
        for copy in [down, *zero]:
            copy.wait()

        @pl.when(i + 1 < 2 * NS)
        def _():
            down, _, zero = weights(i + 1)
            for copy in [down, *zero]:
                copy.start()

        def products(rows):
            return dot_nt(by[rows, :], wdb[slot])

        def elements(rows, by_hid):
            gate = acc[2 * slot, rows, :]
            up = acc[2 * slot + 1, rows, :]
            by_hid = by_hid.astype(BF).astype(F32)
            sig = jax.nn.sigmoid(gate)
            silu = gate * sig
            hid[rows, :] = (silu * up).astype(BF)
            dup[rows, :] = (by_hid * silu).astype(BF)
            dgt[rows, :] = (by_hid * up * (sig * (1.0 + gate * (1.0 - sig)))).astype(BF)

        pipelined(T // TB, TB // H, products, elements)

    def gradient(s, m):
        left, right = ((actt, dgt), (actt, dup), (byt, hid))[m]
        grad[lax.rem(s, GRADS), m] = dot(left[...], right[...])

    def step(h, c):
        in1 = h < STEPS1 * NS
        in0 = (h >= START0) & (h < START0 + STEPS0 * NS)
        h0 = h - START0
        s = jnp.where(in1, lax.div(h, STEPS1), NS + lax.div(h0, STEPS0))
        part = jnp.where(in1, lax.rem(h, STEPS1), lax.rem(h0, STEPS0))

        @pl.when(in1 & (part < 2))
        def _():
            second_layer(s, part)

        @pl.when(h == 2)
        def _():
            loads[2].wait()
            loads[3].wait()

        @pl.when(h == STEPS1 * NS - 1)
        def _():
            h1_load.start()

        @pl.when((h >= STEPS1 * NS) & (h < START0))
        def _():
            between(h - STEPS1 * NS)

        @pl.when(in0 & (part == 0))
        def _():
            first_layer(s)

        @pl.when((in1 & (part == STEPS1 - 2)) | (in0 & (part == 0)))
        def _():
            gradient(s, 0)

        @pl.when((in1 & (part == STEPS1 - 1)) | (in0 & (part == 1)))
        def _():
            gradient(s, 1)
            gradient(s, 2)

        service(h)
        return c

    last = max(START0 + STEPS0 * NS + OFF[6], STEPS1 * NS + OFF[NR], START0 + STEPS0 * Q + OFF[NR])
    lax.fori_loop(0, last, step, 0)
    out = pltpu.make_async_copy(g0b, g0_ref, asem.at[0])
    out.start()
    out.wait()


def backward(a1, dy, a1t, dyt, h1, a0t, gate, up, wg, wu, wd):
    anyspec = pl.BlockSpec(memory_space=pl.ANY)
    V = pltpu.VMEM
    DMA = pltpu.SemaphoreType.DMA
    return pl.pallas_call(
        backward_kernel,
        name="backward",
        in_specs=[anyspec] * 11,
        out_specs=[anyspec] * 2,
        out_shape=[jax.ShapeDtypeStruct((3, NS + Q, D, SL), BF), jax.ShapeDtypeStruct((3, NS - Q, 16, SL), BF)],
        scratch_shapes=[
            V((T, D), BF), V((T, D), BF), V((D, T), BF), V((D, T), BF), V((4, T, SL), F32),
            V((T, SL), BF), V((T, SL), BF), V((T, SL), BF),
            V((2, D, SL), BF), V((2, D, SL), BF), V((2, SL, D), BF),
            V((GRADS, 3, D, SL), F32), V((SLOTS, 3, 256, SL), F32), V((SLOTS, 3, 64, SL), F32),
            *[V((SLOTS, 3, 2, size, width), BF) for size in (256, 64, 16) for width in (128, 128, SL, SL)],
            V((CB, 3, 256, SL), BF), V((3, NS - Q, 16, SL), BF),
            DMA((2, 3)), DMA((4,)), DMA((SEMS, 3)), DMA((NR, SEMS, 3, 2)), DMA((NR, SEMS, 3, 2)),
        ],
        compiler_params=pltpu.CompilerParams(vmem_limit_bytes=VMEM_LIMIT, collective_id=0, has_side_effects=True),
        cost_estimate=pl.CostEstimate(flops=24 * T * D * FF, bytes_accessed=150_000_000, transcendentals=2 * T * FF),
    )(a1, dy, a1t, dyt, h1, a0t, gate, up, wg, wu, wd)


def adam_kernel(gathered, *refs):
    ins, rest = refs[:12], refs[12:]
    if gathered:
        rest = rest[9:]
    outs, rest = rest[:9], rest[9:]
    for m in range(3):
        w_ref, m_ref, v_ref, g_ref = ins[m], ins[3 + m], ins[6 + m], ins[9 + m]
        w_out, m_out, v_out = outs[m], outs[3 + m], outs[6 + m]

        def take(at, g):
            g = g.astype(F32)
            w = w_ref[at].astype(F32)
            mean = 0.9 * m_ref[at] + 0.1 * g
            var = 0.95 * v_ref[at] + 0.05 * g * g
            w_out[at] = (w - 0.02 * (mean * lax.rsqrt(var + 1e-8) + 0.1 * w)).astype(BF)
            m_out[at] = mean
            v_out[at] = var

        if gathered:
            whole = rest[0]
            for n in range(64 // CUT):
                digits = (n // 16, n // 4 % 4, n % 4)
                x, y, z = (digits[(d - m) % 3] for d in range(3))
                whole[n * 16 : n * 16 + 16, :] = g_ref[x, y, z, 0, 0]
            look = lambda rows: whole[rows, :]
        else:
            look = lambda rows: g_ref[0, 0, rows, :]

        if m < 2:

            def one(b, c):
                rows = pl.ds(pl.multiple_of(b * 64, 64), 64)
                take((0, rows, slice(None)), look(rows))
                return c

            lax.fori_loop(0, D // CUT // 64, one, 0)
        else:

            def one(b, c):
                rows = pl.ds(pl.multiple_of(b * 128, 128), 128)
                take((0, slice(None), rows), look(rows).T)
                return c

            lax.fori_loop(0, D // CUT // 128, one, 0)


def adam(first, count, weights, means, variances, gradients, so_far=None):
    rows = D // CUT

    def place(j):
        s = first + j // CUT
        return jnp.where(s < NS, 1, 0), jnp.where(s < NS, s, s - NS), j % CUT

    def at_wide(j):
        layer, column, row = place(j)
        return layer, row, column

    wide = pl.BlockSpec((1, rows, SL), at_wide)
    tall = pl.BlockSpec((1, SL, rows), place)
    mine = [wide, wide, tall]
    gathered = so_far is not None
    if gathered:
        gradients = gradients.reshape(4, 4, 4, *gradients.shape[1:])

        def spec(m):
            return pl.BlockSpec(
                tuple(4 // CUT if d == m else 4 for d in range(3)) + (1, 1, 16, SL),
                lambda j: tuple(j % CUT if d == m else 0 for d in range(3)) + (m, j // CUT, 0, 0),
            )

    else:

        def spec(m):
            return pl.BlockSpec((1, 1, rows, SL), lambda j: (m, j // CUT, j % CUT, 0))

    shapes = [jax.ShapeDtypeStruct(a.shape, a.dtype) for a in (*weights, *means, *variances)]
    return pl.pallas_call(
        functools.partial(adam_kernel, gathered),
        name="adamw_rest" if gathered else "adamw",
        grid=(count * CUT,),
        in_specs=mine * 3 + [spec(m) for m in range(3)] + ([pl.BlockSpec(memory_space=pl.ANY)] * 9 if gathered else []),
        out_specs=mine * 3,
        out_shape=shapes,
        input_output_aliases={12 + k: k for k in range(9)} if gathered else {},
        scratch_shapes=[pltpu.VMEM((rows, SL), BF)] if gathered else [],
        compiler_params=pltpu.CompilerParams(vmem_limit_bytes=VMEM_LIMIT),
        cost_estimate=pl.CostEstimate(flops=10**10, bytes_accessed=66 * D * SL * count, transcendentals=3 * D * SL * count),
    )(*weights, *means, *variances, *[gradients] * 3, *(so_far or ()))


def solution(mesh):
    def step(x, dy, *arrays):
        x, dy = x[0], dy[0]
        weights, means, variances = (arrays[k : k + 3] for k in (0, 3, 6))
        gate, up, h1, a1, a0t, a1t, dyt = forward(x, dy, *weights)
        g1, g0 = backward(a1, dy, a1t, dyt, h1, a0t, gate, up, *weights)
        g0 = lax.all_gather(g0, "dp", axis=0)
        new = adam(0, NS + Q, weights, means, variances, g1)
        return tuple(adam(NS + Q, NS - Q, weights, means, variances, g0, new))

    return jax.shard_map(
        step,
        mesh=mesh,
        in_specs=(P(("rep", "dp"), None, None),) * 2 + (P(None, None, None),) * 9,
        out_specs=(P("rep", None, None),) * 9,
        check_vma=False,
    )
```

time: 630 us -> 574 us (0.911)
  waiting for transfers between devices: 40 us -> 0.04 us
  Pallas kernels: 576 us -> 556 us
    all_gather x1, waiting for transfers between devices: 40 us -> 0.02 us  [step(): g0 = lax.all_gather(g0, 'dp', axis=0)]
    pallas_call x1, Pallas kernels: 342 us -> 321 us  [backward(): pl.pallas_call(backward_kernel, name='backward', in_specs=[anyspec] * 11,...]
    pallas_call x2, Pallas kernels: 159 us -> 166 us  [adam(): pl.pallas_call(functools.partial(adam_kernel, gathered), name='adamw_rest...]
    pallas_call x1, Pallas kernels: 75 us -> 68.4 us  [forward(): pl.pallas_call(forward_kernel, name='forward', grid=(NS,), in_specs=[whol...]
  transfers between devices with their start and end apart: 1 -> 1, of which waited for: 1 -> 0; matrix products, arithmetic and copies ran while one was open for 0% -> 0% of each run, Pallas kernels for 13% -> 18%
where the time goes in v2:
time: 574 us; the launch traced here: 570 us
  Pallas kernels  556 us (97%)
  between operations  14.1 us (2%)
    pallas_call x1, Pallas kernels, backward(): pl.pallas_call(backward_kernel, name='backward', in_specs=[anyspec] * 11,...  321 us
    pallas_call x2, Pallas kernels, adam(): pl.pallas_call(functools.partial(adam_kernel, gathered), name='adamw_rest...  166 us
    pallas_call x1, Pallas kernels, forward(): pl.pallas_call(forward_kernel, name='forward', grid=(NS,), in_specs=[whol...  68.4 us
  transfers between devices with their start and end apart: 1, of which 0 were waited for; matrix products, arithmetic and copies ran while one was open for 0% of the time, Pallas kernels for 18%

profile of v2, /device:TPU:1, one launch (start us, length us, event | category | flops | bytes accessed | tf_op | source)
XLA Modules:
  0.0 570.3 jit_solution(17966339849486232177)
XLA Ops:
  7.2 0.0 all-gather.3.cloned.1.call-start
  7.2 68.4 %forward.1 = (f32[13,2048,256]{2,1,0:T(8,128)}, f32[13,2048,256]{2,1,0:T(8,128)}, bf16[2048,1024]{1,0:T(8,128)(2,1)}, bf16[2048,1024]{1,0:T(8,128)(2,1)}, bf16[1...) custom-call(bf16[2048,1024]{1,0:T(8,128)(2,1)} %bitcast.6, ...), custom_call_target="tpu_custom_call" | custom-call | flops 41875931136 | bytes 100000000 | tf_op jit(solution)/shard_map/forward/pallas_call | solution.py:123
  75.6 321.4 %backward.1 = (bf16[3,16,1024,256]{3,2,1,0:T(8,128)(2,1)}, bf16[3,10,16,256]{3,2,1,0:T(8,128)(2,1)}) custom-call(bf16[2048,1024]{1,0:T(8,128)(2,1)} %get-tuple-element.27.a1_ref, bf16[2048,1024]{1,0:T(8,128)(2,1)} %bitcast.8, bf16[1024,2048]{1,0:T(8,128)(2,1)} %get-tuple-element.28.a1t_ref, bf16[1024,2048]{1,0:T(8,128)(2,1)} %get-tuple-element.29.dyt_ref, ...), custom_call_target="tpu_custom_call" | custom-call | flops 167503724544 | bytes 150000000 | tf_op jit(solution)/shard_map/backward/pallas_call | solution.py:483
  397.0 0.0 all-gather.3.cloned.1.call-update
  397.0 101.9 %adamw.1 = (bf16[2,1024,3328]{2,1,0:T(8,128)(2,1)}, bf16[2,1024,3328]{2,1,0:T(8,128)(2,1)}, bf16[2,3328,1024]{2,1,0:T(8,128)(2,1)}, f32[2,1024,3328]{2,1,0:T(8,1...) custom-call(bf16[2,1024,3328]{2,1,0:T(8,128)(2,1)} %refs_0_.3, ...), custom_call_target="tpu_custom_call" | custom-call | flops 10000000000 | bytes 276824064 | tf_op jit(solution)/shard_map/adamw/pallas_call | solution.py:579
  499.0 0.0 all-gather.3.cloned.1.call-done
  499.0 64.4 %adamw_rest.1 = (bf16[2,1024,3328]{2,1,0:T(8,128)(2,1)}, bf16[2,1024,3328]{2,1,0:T(8,128)(2,1)}, bf16[2,3328,1024]{2,1,0:T(8,128)(2,1)}, f32[2,1024,3328]{2,1,0:...) custom-call(bf16[2,1024,3328]{2,1,0:T(8,128)(2,1)} %refs_0_.3, ...), custom_call_target="tpu_custom_call", output_to_operand_aliasing={{0}: (12, {}), {1}: (13, {}), {2}: (14, {}), {3}: (15, {}),... | custom-call | flops 10000000000 | bytes 173015040 | tf_op jit(solution)/shard_map/adamw_rest/pallas_call | solution.py:579
Async XLA Ops:
  7.2 491.8 %all-gather.3.cloned.1.call-start = ((), (), s32[]{:S(2)}) async-start(), calls=%async_computation | async-start | bytes 15974400 | tf_op jit(solution)/shard_map/all_gather | solution.py:599
Sparse Core Ops, SparseCore 0:
  397.2 101.7 all-gather.2

commit v3 on v2

--- a/solution.py
+++ b/solution.py
@@ -11,7 +11,8 @@
 NS = FF // SL
 TB = 512
 H = 256
-FB, FH = 2048, 512
+FH = 512
+PIECES = 8
 F32, BF = jnp.float32, jnp.bfloat16
 MESH = pl.DeviceIdType.MESH
 VMEM_LIMIT = 66_900_000
@@ -20,9 +21,9 @@
 START0 = STEPS1 * NS + MID
 OFF = (0, 2, 5, 7, 9, 11, 13, 15, 17, 20, 23, 29, 32)
 NR = 12
-SLOTS, SEMS, GRADS, CB = 4, 4, 4, 8
+SLOTS, SEMS, CB = 4, 4, 8
 Q = 3
-CUT = 2
+CUT = 1
 
 
 def dot(a, b):
@@ -56,103 +57,12 @@
     lax.fori_loop(0, count, one, 0)
 
 
-def forward_kernel(x_ref, dy_ref, wg_ref, wu_ref, wd_ref, gate_ref, up_ref, h1_ref, a1_ref, a0t_ref, a1t_ref, dyt_ref, a0, acc, stage, sem):
-    j = pl.program_id(0)
-
-    @pl.when(j == 0)
-    def _():
-        def one(b, c):
-            rows = pl.ds(pl.multiple_of(b * TB, TB), TB)
-            a = normed(x_ref[rows, :])
-            a0[rows, :] = a
-            acc[rows, :] = jnp.zeros((TB, D), F32)
-            return c
-
-        lax.fori_loop(0, T // TB, one, 0)
-
-    def transposed(src, dst):
-        def one(b, c):
-            rows = pl.ds(pl.multiple_of(b * TB, TB), TB)
-            stage[:, rows] = src[rows, :].T
-            return c
-
-        lax.fori_loop(0, T // TB, one, 0)
-        copy = pltpu.make_async_copy(stage, dst, sem)
-        copy.start()
-        copy.wait()
-
-    @pl.when(j == 1)
-    def _():
-        transposed(a0, a0t_ref)
-
-    @pl.when(j == 2)
-    def _():
-        transposed(dy_ref, dyt_ref)
-
-    def gate_up(rows):
-        a = a0[rows, :]
-        return dot(a, wg_ref[0]), dot(a, wu_ref[0])
-
-    def hidden(rows, gate, up):
-        gate_ref[0, rows, :] = gate
-        up_ref[0, rows, :] = up
-        return (gate * jax.nn.sigmoid(gate) * up).astype(BF)
-
-    def down(rows, hid):
-        acc[rows, :] += dot(hid, wd_ref[0])
-
-    pipelined(T // FB, FB // FH, gate_up, hidden, down)
-
-    @pl.when(j == NS - 1)
-    def _():
-        def one(b, c):
-            rows = pl.ds(pl.multiple_of(b * TB, TB), TB)
-            h1 = (x_ref[rows, :].astype(F32) + acc[rows, :].astype(BF).astype(F32)).astype(BF)
-            h1_ref[rows, :] = h1
-            a1_ref[rows, :] = normed(h1)
-            return c
-
-        lax.fori_loop(0, T // TB, one, 0)
-        transposed(a1_ref, a1t_ref)
-
-
-def forward(x, dy, wg, wu, wd):
-    whole = pl.BlockSpec((T, D), lambda j: (0, 0))
-    wide = pl.BlockSpec((1, T, SL), lambda j: (j, 0, 0))
-    anyspec = pl.BlockSpec(memory_space=pl.ANY)
-    return pl.pallas_call(
-        forward_kernel,
-        name="forward",
-        grid=(NS,),
-        in_specs=[
-            whole,
-            whole,
-            pl.BlockSpec((1, D, SL), lambda j: (0, 0, j)),
-            pl.BlockSpec((1, D, SL), lambda j: (0, 0, j)),
-            pl.BlockSpec((1, SL, D), lambda j: (0, j, 0)),
-        ],
-        out_specs=[wide, wide, whole, whole, anyspec, anyspec, anyspec],
-        out_shape=[
-            jax.ShapeDtypeStruct((NS, T, SL), F32),
-            jax.ShapeDtypeStruct((NS, T, SL), F32),
-            jax.ShapeDtypeStruct((T, D), BF),
-            jax.ShapeDtypeStruct((T, D), BF),
-            jax.ShapeDtypeStruct((D, T), BF),
-            jax.ShapeDtypeStruct((D, T), BF),
-            jax.ShapeDtypeStruct((D, T), BF),
-        ],
-        scratch_shapes=[pltpu.VMEM((T, D), BF), pltpu.VMEM((T, D), F32), pltpu.VMEM((D, T), BF), pltpu.SemaphoreType.DMA],
-        compiler_params=pltpu.CompilerParams(vmem_limit_bytes=VMEM_LIMIT),
-        cost_estimate=pl.CostEstimate(flops=6 * T * D * FF, bytes_accessed=100_000_000, transcendentals=T * FF),
-    )(x, dy, wg, wu, wd)
-
-
-def backward_kernel(
-    a1_ref, dy_ref, a1t_ref, dyt_ref, h1_ref, a0t_ref, gate_ref, up_ref, wg_ref, wu_ref, wd_ref,
-    g1_ref, g0_ref,
+def step_kernel(
+    x_ref, dy_ref, wg_ref, wu_ref, wd_ref,
+    g1_ref, g0_ref, gate_ref, up_ref, h1_ref, a0t_ref,
     act, by, actt, byt, acc, hid, dgt, dup, wgb, wub, wdb,
     grad, s1, s2, sa0, ra0, sb0, rb0, sa1, ra1, sb1, rb1, sa2, ra2, sb2, rb2, cb, g0b,
-    wsem, asem, lsem, send, recv,
+    wsem, asem, osem, lsem, send, recv,
 ):
     me = lax.axis_index("dp")
     xyz = (lax.div(me, 16), lax.rem(lax.div(me, 4), 4), lax.rem(me, 4))
@@ -173,7 +83,6 @@
     for d in range(3):
         for n in (plus[d], minus[d]):
             pl.semaphore_signal(barrier, inc=1, device_id={"dp": n}, device_id_type=MESH)
-    pl.semaphore_wait(barrier, 6)
 
     HALF = (pl.ds(0, 128), pl.ds(128, 128))
     sas, ras, sbs, rbs = (sa0, sa1, sa2), (ra0, ra1, ra2), (sb0, sb1, sb2), (rb0, rb1, rb2)
@@ -218,12 +127,13 @@
         )
 
     def total(ph, s):
-        return grad.at[lax.rem(s, GRADS)] if ph == 0 else (s1, s2)[ph - 1].at[lax.rem(s, SLOTS)]
+        return grad.at[pl.ds(pl.multiple_of(4 * lax.rem(s, 2), 4), 4)] if ph == 0 else (s1, s2)[ph - 1].at[lax.rem(s, SLOTS)]
 
     def mine(ph, s, m):
         slot = lax.rem(s, SLOTS)
         rows = block(digit[m][ph], sizes[ph])
-        return total(ph, s)[m, rows, :] + rbs[ph][slot, m, 0].astype(F32) + rbs[ph][slot, m, 1].astype(F32)
+        so_far = s1[slot, m] if ph == 0 else total(ph, s)[m, rows, :]
+        return so_far + rbs[ph][slot, m, 0].astype(F32) + rbs[ph][slot, m, 1].astype(F32)
 
     def prepare(r, s):
         slot = lax.rem(s, SLOTS)
@@ -244,6 +154,8 @@
                     add, keep = HALF[k], HALF[1 - k]
                     sbs[ph][slot, m, k, :, add] = (total(ph, s)[m, near, add] + ras[ph][slot, m, k].astype(F32)).astype(BF)
                     sbs[ph][slot, m, k, :, keep] = total(ph, s)[m, near, keep].astype(BF)
+            if r == 1:
+                s1[slot, m] = total(0, s)[m, block(digit[m][0], 256), :]
             if r == 6:
                 done = mine(2, s, m).astype(BF)
 
@@ -268,22 +180,35 @@
     def service(h):
         q1, r1 = lax.div(h, STEPS1), lax.rem(h, STEPS1)
         q0, r0 = lax.div(h, STEPS0), lax.rem(h, STEPS0)
-        todo = []
-        for r in (2, 3, 4, 5, 0, 1, 6, 7, 8, 9, 10, 11, 12):
-            from1, from0 = STEPS1 - 1 + OFF[r], START0 + STEPS0 - 1 + OFF[r]
-            one = (r1 == from1 % STEPS1) & (h >= from1) & (h < from1 + STEPS1 * NS)
-
-            def zero(count):
-                return (r0 == from0 % STEPS0) & (h >= from0) & (h < from0 + STEPS0 * count)
-
-            s = jnp.where(h >= from0, NS + q0 - from0 // STEPS0, q1 - from1 // STEPS1)
-            prepared = one | zero(NS if r <= 6 else Q)
-            todo.append((r, s, prepared, one | zero(Q) if r == 6 else prepared))
-        for r, s, prepared, _ in todo:
-            pl.when(prepared)(functools.partial(prepare, r, s))
-        for r, s, _, sent in todo:
-            if r < NR:
-                pl.when(sent)(functools.partial(start, r, s))
+
+        def some(parity):
+            todo = []
+            for r in (2, 3, 4, 5, 0, 1, 6, 7, 8, 9, 10, 11, 12):
+                from1, from0 = STEPS1 - 1 + OFF[r], START0 + STEPS0 - 1 + OFF[r]
+                if from1 % 2 != parity:
+                    continue
+                one = (r1 == from1 % STEPS1) & (h >= from1) & (h < from1 + STEPS1 * NS)
+
+                def zero(count):
+                    return (r0 == from0 % STEPS0) & (h >= from0) & (h < from0 + STEPS0 * count)
+
+                s = jnp.where(h >= from0, NS + q0 - from0 // STEPS0, q1 - from1 // STEPS1)
+                prepared = one | zero(NS if r <= 6 else Q)
+                todo.append((r, s, prepared, one | zero(Q) if r == 6 else prepared))
+            for r, s, prepared, _ in todo:
+                if r <= 6:
+                    pl.when(prepared)(functools.partial(prepare, r, s))
+            for r, s, _, sent in todo:
+
+                @pl.when(sent)
+                def _():
+                    if r > 6:
+                        prepare(r, s)
+                    if r < NR:
+                        start(r, s)
+
+        for parity in range(2):
+            pl.when(lax.rem(h, 2) == parity)(functools.partial(some, parity))
 
     def weights(i):
         slot = lax.rem(i, 2)
@@ -301,25 +226,119 @@
         ]
         return down, one, zero
 
-    loads = [
-        pltpu.make_async_copy(a1_ref, act, asem.at[0]),
-        pltpu.make_async_copy(dy_ref, by, asem.at[1]),
-        pltpu.make_async_copy(a1t_ref, actt, asem.at[2]),
-        pltpu.make_async_copy(dyt_ref, byt, asem.at[3]),
-    ]
-    down, one, _ = weights(0)
-    for copy in [down, *one, *loads]:
+    def first_weights(j):
+        slot, columns = lax.rem(j, 2), block(j, SL)
+        return [
+            pltpu.make_async_copy(wg_ref.at[0, :, columns], wgb.at[slot], wsem.at[slot, 0]),
+            pltpu.make_async_copy(wu_ref.at[0, :, columns], wub.at[slot], wsem.at[slot, 1]),
+            pltpu.make_async_copy(wd_ref.at[0, columns, :], wdb.at[slot], wsem.at[slot, 2]),
+        ]
+
+    def kept(j):
+        slot = lax.rem(j, 2)
+        return [
+            pltpu.make_async_copy(grad.at[4 * slot + 2 * k + half], ref.at[j, pl.ds(half * D, D)], osem.at[slot, k, half])
+            for k, ref in enumerate((gate_ref, up_ref))
+            for half in range(2)
+        ]
+
+    x_load = pltpu.make_async_copy(x_ref, act, asem.at[0])
+    dy_load = pltpu.make_async_copy(dy_ref, by, asem.at[1])
+    for copy in [x_load, *first_weights(0), dy_load]:
         copy.start()
 
-    def clear(b, c):
-        rows = block(b, TB)
+    def clear(rows):
         for n in range(4):
             acc[n, rows, :] = jnp.zeros((TB, SL), F32)
+
+    x_load.wait()
+
+    def enter(b, c):
+        rows = block(b, TB)
+        act[rows, :] = normed(act[rows, :])
+        clear(rows)
         return c
 
-    lax.fori_loop(0, T // TB, clear, 0)
-    loads[0].wait()
-    loads[1].wait()
+    lax.fori_loop(0, T // TB, enter, 0)
+    dy_load.wait()
+
+    def forward(j, c):
+        slot = lax.rem(j, 2)
+        for copy in first_weights(j):
+            copy.wait()
+
+        @pl.when(j + 1 < NS)
+        def _():
+            for copy in first_weights(j + 1):
+                copy.start()
+
+        @pl.when(j >= 2)
+        def _():
+            for copy in kept(j - 2):
+                copy.wait()
+
+        piece = block(jnp.minimum(j, PIECES - 1), T // PIECES)
+        actt[:, piece] = act[piece, :].T
+        byt[:, piece] = by[piece, :].T
+
+        def gate_up(p):
+            a = act[p * FH : p * FH + FH, :]
+            return dot(a, wgb[slot]), dot(a, wub[slot])
+
+        def hidden(p, gate, up):
+            half, at = divmod(p * FH, D)
+            grad[4 * slot + half, at : at + FH, :] = gate
+            grad[4 * slot + 2 + half, at : at + FH, :] = up
+            return ((gate * jax.nn.sigmoid(gate) * up).astype(BF),)
+
+        def down(p, hidden):
+            for n in range(4):
+                acc[n, p * FH : p * FH + FH, :] += dot(hidden, wdb[slot, :, n * SL : n * SL + SL])
+
+        parts = T // FH
+        values = [()] * parts
+        for at in range(parts + 2):
+            for k, work in enumerate((gate_up, hidden, down)):
+                if 0 <= at - k < parts:
+                    values[at - k] = work(at - k, *values[at - k])
+        for copy in kept(j):
+            copy.start()
+        return c
+
+    lax.fori_loop(0, NS, forward, 0)
+    a0t_keep = pltpu.make_async_copy(actt, a0t_ref, asem.at[2])
+    again = pltpu.make_async_copy(x_ref, act, asem.at[0])
+    a0t_keep.start()
+    again.start()
+    down, one, _ = weights(0)
+    for copy in [down, *one]:
+        copy.start()
+    for copy in [*kept(NS - 2), *kept(NS - 1)]:
+        copy.wait()
+    a0t_keep.wait()
+    again.wait()
+    h1_keep = pltpu.make_async_copy(act, h1_ref, asem.at[1])
+
+    def leave(b, c):
+        rows = block(b, TB)
+        added = jnp.concatenate([acc[n, rows, :] for n in range(4)], axis=1).astype(BF)
+        act[rows, :] = (act[rows, :].astype(F32) + added.astype(F32)).astype(BF)
+        clear(rows)
+        return c
+
+    lax.fori_loop(0, T // TB, leave, 0)
+    h1_keep.start()
+    h1_keep.wait()
+
+    def enter_second(b, c):
+        rows = block(b, TB)
+        a1 = normed(act[rows, :])
+        act[rows, :] = a1
+        actt[:, rows] = a1.T
+        return c
+
+    lax.fori_loop(0, T // TB, enter_second, 0)
+    pl.semaphore_wait(barrier, 6)
     h1_load = pltpu.make_async_copy(h1_ref, act, asem.at[0])
     a0t_load = pltpu.make_async_copy(a0t_ref, actt, asem.at[2])
 
@@ -427,7 +446,7 @@
 
     def gradient(s, m):
         left, right = ((actt, dgt), (actt, dup), (byt, hid))[m]
-        grad[lax.rem(s, GRADS), m] = dot(left[...], right[...])
+        grad[4 * lax.rem(s, 2) + m] = dot(left[...], right[...])
 
     def step(h, c):
         in1 = h < STEPS1 * NS
@@ -440,11 +459,6 @@
         def _():
             second_layer(s, part)
 
-        @pl.when(h == 2)
-        def _():
-            loads[2].wait()
-            loads[3].wait()
-
         @pl.when(h == STEPS1 * NS - 1)
         def _():
             h1_load.start()
@@ -476,28 +490,35 @@
     out.wait()
 
 
-def backward(a1, dy, a1t, dyt, h1, a0t, gate, up, wg, wu, wd):
+def gradients(x, dy, wg, wu, wd):
     anyspec = pl.BlockSpec(memory_space=pl.ANY)
     V = pltpu.VMEM
     DMA = pltpu.SemaphoreType.DMA
     return pl.pallas_call(
-        backward_kernel,
-        name="backward",
-        in_specs=[anyspec] * 11,
-        out_specs=[anyspec] * 2,
-        out_shape=[jax.ShapeDtypeStruct((3, NS + Q, D, SL), BF), jax.ShapeDtypeStruct((3, NS - Q, 16, SL), BF)],
+        step_kernel,
+        name="gradients",
+        in_specs=[anyspec] * 5,
+        out_specs=[anyspec] * 6,
+        out_shape=[
+            jax.ShapeDtypeStruct((3, NS + Q, D, SL), BF),
+            jax.ShapeDtypeStruct((3, NS - Q, 16, SL), BF),
+            jax.ShapeDtypeStruct((NS, T, SL), F32),
+            jax.ShapeDtypeStruct((NS, T, SL), F32),
+            jax.ShapeDtypeStruct((T, D), BF),
+            jax.ShapeDtypeStruct((D, T), BF),
+        ],
         scratch_shapes=[
             V((T, D), BF), V((T, D), BF), V((D, T), BF), V((D, T), BF), V((4, T, SL), F32),
             V((T, SL), BF), V((T, SL), BF), V((T, SL), BF),
             V((2, D, SL), BF), V((2, D, SL), BF), V((2, SL, D), BF),
-            V((GRADS, 3, D, SL), F32), V((SLOTS, 3, 256, SL), F32), V((SLOTS, 3, 64, SL), F32),
+            V((8, D, SL), F32), V((SLOTS, 3, 256, SL), F32), V((SLOTS, 3, 64, SL), F32),
             *[V((SLOTS, 3, 2, size, width), BF) for size in (256, 64, 16) for width in (128, 128, SL, SL)],
             V((CB, 3, 256, SL), BF), V((3, NS - Q, 16, SL), BF),
-            DMA((2, 3)), DMA((4,)), DMA((SEMS, 3)), DMA((NR, SEMS, 3, 2)), DMA((NR, SEMS, 3, 2)),
+            DMA((2, 3)), DMA((4,)), DMA((2, 2, 2)), DMA((SEMS, 3)), DMA((NR, SEMS, 3, 2)), DMA((NR, SEMS, 3, 2)),
         ],
         compiler_params=pltpu.CompilerParams(vmem_limit_bytes=VMEM_LIMIT, collective_id=0, has_side_effects=True),
-        cost_estimate=pl.CostEstimate(flops=24 * T * D * FF, bytes_accessed=150_000_000, transcendentals=2 * T * FF),
-    )(a1, dy, a1t, dyt, h1, a0t, gate, up, wg, wu, wd)
+        cost_estimate=pl.CostEstimate(flops=30 * T * D * FF, bytes_accessed=250_000_000, transcendentals=3 * T * FF),
+    )(x, dy, wg, wu, wd)[:2]
 
 
 def adam_kernel(gathered, *refs):
@@ -594,8 +615,7 @@
     def step(x, dy, *arrays):
         x, dy = x[0], dy[0]
         weights, means, variances = (arrays[k : k + 3] for k in (0, 3, 6))
-        gate, up, h1, a1, a0t, a1t, dyt = forward(x, dy, *weights)
-        g1, g0 = backward(a1, dy, a1t, dyt, h1, a0t, gate, up, *weights)
+        g1, g0 = gradients(x, dy, *weights)
         g0 = lax.all_gather(g0, "dp", axis=0)
         new = adam(0, NS + Q, weights, means, variances, g1)
         return tuple(adam(NS + Q, NS - Q, weights, means, variances, g0, new))

time: 574 us -> 537 us (0.936)
  Pallas kernels: 556 us -> 515 us
  waiting for transfers between devices: 0.04 us -> 7.31 us
    pallas_call x2 -> x1, Pallas kernels: 390 us -> 363 us  [gradients(): pl.pallas_call(step_kernel, name='gradients', in_specs=[anyspec] * 5, out...]
    pallas_call x2, Pallas kernels: 166 us -> 153 us  [adam(): pl.pallas_call(functools.partial(adam_kernel, gathered), name='adamw_rest...]
    all_gather x1, waiting for transfers between devices: 0.02 us -> 7.29 us  [step(): g0 = lax.all_gather(g0, 'dp', axis=0)]
  transfers between devices with their start and end apart: 1 -> 1, of which waited for: 0 -> 1; matrix products, arithmetic and copies ran while one was open for 0% -> 0% of each run, Pallas kernels for 18% -> 17%
where the time goes in v3:
time: 537 us
  Pallas kernels  515 us (96%)
  between operations  14.1 us (3%)
  waiting for transfers between devices  7.31 us (1%)
    pallas_call x1, Pallas kernels, gradients(): pl.pallas_call(step_kernel, name='gradients', in_specs=[anyspec] * 5, out...  363 us
    pallas_call x2, Pallas kernels, adam(): pl.pallas_call(functools.partial(adam_kernel, gathered), name='adamw_rest...  153 us
  transfers between devices with their start and end apart: 1, of which 1 were waited for; matrix products, arithmetic and copies ran while one was open for 0% of the time, Pallas kernels for 17%

profile of v3, /device:TPU:1, one launch (start us, length us, event | category | flops | bytes accessed | tf_op | source)
XLA Modules:
  0.0 536.8 jit_solution(7426547136881285309)
XLA Ops:
  7.2 0.0 all-gather.3.cloned.1.call-start
  7.2 362.6 %gradients.1 = (bf16[3,16,1024,256]{3,2,1,0:T(8,128)(2,1)}, bf16[3,10,16,256]{3,2,1,0:T(8,128)(2,1)}, f32[13,2048,256]{2,1,0:T(8,128)}, f32[13,2048,256]{2,1,0:T...) custom-call(bf16[2048,1024]{1,0:T(8,128)(2,1)} %bitcast.6, bf16[2048,1024]{1,0:T(8,128)(2,1)} %bitcast.7, ...), custom_call_target="tpu_custom_call" | custom-call | flops 209379655680 | bytes 250000000 | tf_op jit(solution)/shard_map/gradients/pallas_call | solution.py:497
  369.8 0.0 all-gather.3.cloned.1.call-update
  369.8 93.6 %adamw.1 = (bf16[2,1024,3328]{2,1,0:T(8,128)(2,1)}, bf16[2,1024,3328]{2,1,0:T(8,128)(2,1)}, bf16[2,3328,1024]{2,1,0:T(8,128)(2,1)}, f32[2,1024,3328]{2,1,0:T(8,1...) custom-call(bf16[2,1024,3328]{2,1,0:T(8,128)(2,1)} %refs_0_.3, ...), custom_call_target="tpu_custom_call" | custom-call | flops 10000000000 | bytes 276824064 | tf_op jit(solution)/shard_map/adamw/pallas_call | solution.py:600
  463.4 7.3 %all-gather.3.cloned.1.call-done = bf16[192,10,16,256]{3,2,1,0:T(8,128)(2,1)} async-done(((bf16[3,10,16,256]{3,2,1,0:T(8,128)(2,1)}), bf16[192,10,16,256]{3,2,1,0:T(8,128)(2,1)}) %all-gather.3.cloned.1.call-update) | async-done | bytes 15728656 | tf_op jit(solution)/shard_map/all_gather | solution.py:619
  470.7 59.2 %adamw_rest.1 = (bf16[2,1024,3328]{2,1,0:T(8,128)(2,1)}, bf16[2,1024,3328]{2,1,0:T(8,128)(2,1)}, bf16[2,3328,1024]{2,1,0:T(8,128)(2,1)}, f32[2,1024,3328]{2,1,0:...) custom-call(bf16[2,1024,3328]{2,1,0:T(8,128)(2,1)} %refs_0_.3, ...), custom_call_target="tpu_custom_call", output_to_operand_aliasing={{0}: (12, {}), {1}: (13, {}), {2}: (14, {}), {3}: (15, {}),... | custom-call | flops 10000000000 | bytes 173015040 | tf_op jit(solution)/shard_map/adamw_rest/pallas_call | solution.py:600
Async XLA Ops:
  7.2 463.5 %all-gather.3.cloned.1.call-start = ((), (), s32[]{:S(2)}) async-start(), calls=%async_computation | async-start | bytes 15974400 | tf_op jit(solution)/shard_map/all_gather | solution.py:619
Sparse Core Ops, SparseCore 0:
  370.0 100.7 all-gather.2

commit v4 on v3

--- a/solution.py
+++ b/solution.py
@@ -19,7 +19,8 @@
 
 STEPS1, MID, STEPS0 = 4, 4, 2
 START0 = STEPS1 * NS + MID
-OFF = (0, 2, 5, 7, 9, 11, 13, 15, 17, 20, 23, 29, 32)
+OFF1 = (0, 2, 5, 7, 9, 11, 13, 15, 17, 20, 23, 26, 29)
+OFF0 = (0, 2, 5, 7, 9, 11, 15, 17, 21, 24, 27, 30, 33)
 NR = 12
 SLOTS, SEMS, CB = 4, 4, 8
 Q = 3
@@ -62,7 +63,7 @@
     g1_ref, g0_ref, gate_ref, up_ref, h1_ref, a0t_ref,
     act, by, actt, byt, acc, hid, dgt, dup, wgb, wub, wdb,
     grad, s1, s2, sa0, ra0, sb0, rb0, sa1, ra1, sb1, rb1, sa2, ra2, sb2, rb2, cb, g0b,
-    wsem, asem, osem, lsem, send, recv,
+    wsem, asem, osem, xsem, lsem, send, recv,
 ):
     me = lax.axis_index("dp")
     xyz = (lax.div(me, 16), lax.rem(lax.div(me, 4), 4), lax.rem(me, 4))
@@ -184,7 +185,7 @@
         def some(parity):
             todo = []
             for r in (2, 3, 4, 5, 0, 1, 6, 7, 8, 9, 10, 11, 12):
-                from1, from0 = STEPS1 - 1 + OFF[r], START0 + STEPS0 - 1 + OFF[r]
+                from1, from0 = STEPS1 - 1 + OFF1[r], START0 + STEPS0 - 1 + OFF0[r]
                 if from1 % 2 != parity:
                     continue
                 one = (r1 == from1 % STEPS1) & (h >= from1) & (h < from1 + STEPS1 * NS)
@@ -253,6 +254,19 @@
 
     x_load.wait()
 
+    columns = [ref.at[...] for ref in (hid, dgt, dup)]
+    lasts = [sb0.at[b // 6, b % 6 // 2, b % 2] for b in range(T // H)]
+    last_columns = pl.ds(3 * SL, SL)
+
+    def moves(ref, out):
+        pairs = [(part, ref.at[:, pl.ds(n * SL, SL)]) for n, part in enumerate(columns)]
+        pairs += [(part, ref.at[pl.ds(b * H, H), last_columns]) for b, part in enumerate(lasts)]
+        return [pltpu.make_async_copy(*(pair if out else pair[::-1]), xsem.at[n]) for n, pair in enumerate(pairs)]
+
+    again = moves(x_ref, False)
+    for copy in again:
+        copy.start()
+
     def enter(b, c):
         rows = block(b, TB)
         act[rows, :] = normed(act[rows, :])
@@ -307,37 +321,34 @@
 
     lax.fori_loop(0, NS, forward, 0)
     a0t_keep = pltpu.make_async_copy(actt, a0t_ref, asem.at[2])
-    again = pltpu.make_async_copy(x_ref, act, asem.at[0])
     a0t_keep.start()
-    again.start()
     down, one, _ = weights(0)
     for copy in [down, *one]:
         copy.start()
-    for copy in [*kept(NS - 2), *kept(NS - 1)]:
+    for copy in [*kept(NS - 2), *kept(NS - 1), *again]:
         copy.wait()
+    for b in range(T // H):
+        rows = pl.ds(b * H, H)
+        pieces = [part.at[rows] for part in columns] + [lasts[b]]
+        h1 = []
+        for n, part in enumerate(pieces):
+            h1.append((part[...].astype(F32) + acc[n, rows, :].astype(BF).astype(F32)).astype(BF))
+            part[...] = h1[n]
+            acc[n, rows, :] = jnp.zeros((H, SL), F32)
+        act[rows, :] = normed(jnp.concatenate(h1, axis=1))
     a0t_keep.wait()
-    again.wait()
-    h1_keep = pltpu.make_async_copy(act, h1_ref, asem.at[1])
-
-    def leave(b, c):
-        rows = block(b, TB)
-        added = jnp.concatenate([acc[n, rows, :] for n in range(4)], axis=1).astype(BF)
-        act[rows, :] = (act[rows, :].astype(F32) + added.astype(F32)).astype(BF)
-        clear(rows)
+    keep = moves(h1_ref, True)
+    for copy in keep:
+        copy.start()
+
+    def turned(b, c):
+        rows = block(b, H)
+        actt[:, rows] = act[rows, :].T
         return c
 
-    lax.fori_loop(0, T // TB, leave, 0)
-    h1_keep.start()
-    h1_keep.wait()
-
-    def enter_second(b, c):
-        rows = block(b, TB)
-        a1 = normed(act[rows, :])
-        act[rows, :] = a1
-        actt[:, rows] = a1.T
-        return c
-
-    lax.fori_loop(0, T // TB, enter_second, 0)
+    lax.fori_loop(0, T // H, turned, 0)
+    for copy in keep:
+        copy.wait()
     pl.semaphore_wait(barrier, 6)
     h1_load = pltpu.make_async_copy(h1_ref, act, asem.at[0])
     a0t_load = pltpu.make_async_copy(a0t_ref, actt, asem.at[2])
@@ -455,21 +466,25 @@
         s = jnp.where(in1, lax.div(h, STEPS1), NS + lax.div(h0, STEPS0))
         part = jnp.where(in1, lax.rem(h, STEPS1), lax.rem(h0, STEPS0))
 
-        @pl.when(in1 & (part < 2))
-        def _():
-            second_layer(s, part)
-
-        @pl.when(h == STEPS1 * NS - 1)
-        def _():
-            h1_load.start()
-
-        @pl.when((h >= STEPS1 * NS) & (h < START0))
-        def _():
-            between(h - STEPS1 * NS)
-
-        @pl.when(in0 & (part == 0))
-        def _():
-            first_layer(s)
+        @pl.when(in1)
+        def _():
+            @pl.when(part < 2)
+            def _():
+                second_layer(s, part)
+
+            @pl.when(h == STEPS1 * NS - 1)
+            def _():
+                h1_load.start()
+
+        @pl.when(h >= STEPS1 * NS)
+        def _():
+            @pl.when(h < START0)
+            def _():
+                between(h - STEPS1 * NS)
+
+            @pl.when(in0 & (part == 0))
+            def _():
+                first_layer(s)
 
         @pl.when((in1 & (part == STEPS1 - 2)) | (in0 & (part == 0)))
         def _():
@@ -483,7 +498,7 @@
         service(h)
         return c
 
-    last = max(START0 + STEPS0 * NS + OFF[6], STEPS1 * NS + OFF[NR], START0 + STEPS0 * Q + OFF[NR])
+    last = max(START0 + STEPS0 * NS + OFF0[6], STEPS1 * NS + OFF1[NR], START0 + STEPS0 * Q + OFF0[NR])
     lax.fori_loop(0, last, step, 0)
     out = pltpu.make_async_copy(g0b, g0_ref, asem.at[0])
     out.start()
@@ -514,7 +529,7 @@
             V((8, D, SL), F32), V((SLOTS, 3, 256, SL), F32), V((SLOTS, 3, 64, SL), F32),
             *[V((SLOTS, 3, 2, size, width), BF) for size in (256, 64, 16) for width in (128, 128, SL, SL)],
             V((CB, 3, 256, SL), BF), V((3, NS - Q, 16, SL), BF),
-            DMA((2, 3)), DMA((4,)), DMA((2, 2, 2)), DMA((SEMS, 3)), DMA((NR, SEMS, 3, 2)), DMA((NR, SEMS, 3, 2)),
+            DMA((2, 3)), DMA((4,)), DMA((2, 2, 2)), DMA((11,)), DMA((SEMS, 3)), DMA((NR, SEMS, 3, 2)), DMA((NR, SEMS, 3, 2)),
         ],
         compiler_params=pltpu.CompilerParams(vmem_limit_bytes=VMEM_LIMIT, collective_id=0, has_side_effects=True),
         cost_estimate=pl.CostEstimate(flops=30 * T * D * FF, bytes_accessed=250_000_000, transcendentals=3 * T * FF),

time: 537 us -> 530 us (0.987)
  Pallas kernels: 515 us -> 508 us
    pallas_call x1, Pallas kernels: 363 us -> 355 us  [gradients(): pl.pallas_call(step_kernel, name='gradients', in_specs=[anyspec] * 5, out...]
  transfers between devices with their start and end apart: 1 -> 1, of which waited for: 1 -> 1; matrix products, arithmetic and copies ran while one was open for 0% -> 0% of each run, Pallas kernels for 17% -> 18%
where the time goes in v4:
time: 530 us
  Pallas kernels  508 us (96%)
  between operations  14.1 us (3%)
  waiting for transfers between devices  7.85 us (1%)
    pallas_call x1, Pallas kernels, gradients(): pl.pallas_call(step_kernel, name='gradients', in_specs=[anyspec] * 5, out...  355 us
    pallas_call x2, Pallas kernels, adam(): pl.pallas_call(functools.partial(adam_kernel, gathered), name='adamw_rest...  153 us
  transfers between devices with their start and end apart: 1, of which 1 were waited for; matrix products, arithmetic and copies ran while one was open for 0% of the time, Pallas kernels for 18%

profile of v4, /device:TPU:1, one launch (start us, length us, event | category | flops | bytes accessed | tf_op | source)
XLA Modules:
  0.0 529.7 jit_solution(285002079277867476)
XLA Ops:
  7.2 0.0 all-gather.3.cloned.1.call-start
  7.2 354.9 %gradients.1 = (bf16[3,16,1024,256]{3,2,1,0:T(8,128)(2,1)}, bf16[3,10,16,256]{3,2,1,0:T(8,128)(2,1)}, f32[13,2048,256]{2,1,0:T(8,128)}, f32[13,2048,256]{2,1,0:T...) custom-call(bf16[2048,1024]{1,0:T(8,128)(2,1)} %bitcast.6, bf16[2048,1024]{1,0:T(8,128)(2,1)} %bitcast.7, ...), custom_call_target="tpu_custom_call" | custom-call | flops 209379655680 | bytes 250000000 | tf_op jit(solution)/shard_map/gradients/pallas_call | solution.py:512
  362.1 0.0 all-gather.3.cloned.1.call-update
  362.1 93.6 %adamw.1 = (bf16[2,1024,3328]{2,1,0:T(8,128)(2,1)}, bf16[2,1024,3328]{2,1,0:T(8,128)(2,1)}, bf16[2,3328,1024]{2,1,0:T(8,128)(2,1)}, f32[2,1024,3328]{2,1,0:T(8,1...) custom-call(bf16[2,1024,3328]{2,1,0:T(8,128)(2,1)} %refs_0_.3, ...), custom_call_target="tpu_custom_call" | custom-call | flops 10000000000 | bytes 276824064 | tf_op jit(solution)/shard_map/adamw/pallas_call | solution.py:615
  455.7 7.8 %all-gather.3.cloned.1.call-done = bf16[192,10,16,256]{3,2,1,0:T(8,128)(2,1)} async-done(((bf16[3,10,16,256]{3,2,1,0:T(8,128)(2,1)}), bf16[192,10,16,256]{3,2,1,0:T(8,128)(2,1)}) %all-gather.3.cloned.1.call-update) | async-done | bytes 15728656 | tf_op jit(solution)/shard_map/all_gather | solution.py:634
  463.6 59.2 %adamw_rest.1 = (bf16[2,1024,3328]{2,1,0:T(8,128)(2,1)}, bf16[2,1024,3328]{2,1,0:T(8,128)(2,1)}, bf16[2,3328,1024]{2,1,0:T(8,128)(2,1)}, f32[2,1024,3328]{2,1,0:...) custom-call(bf16[2,1024,3328]{2,1,0:T(8,128)(2,1)} %refs_0_.3, ...), custom_call_target="tpu_custom_call", output_to_operand_aliasing={{0}: (12, {}), {1}: (13, {}), {2}: (14, {}), {3}: (15, {}),... | custom-call | flops 10000000000 | bytes 173015040 | tf_op jit(solution)/shard_map/adamw_rest/pallas_call | solution.py:615
Async XLA Ops:
  7.2 456.4 %all-gather.3.cloned.1.call-start = ((), (), s32[]{:S(2)}) async-start(), calls=%async_computation | async-start | bytes 15974400 | tf_op jit(solution)/shard_map/all_gather | solution.py:634
Sparse Core Ops, SparseCore 0:
  362.3 101.2 all-gather.2

commit v5 on v4

--- a/solution.py
+++ b/solution.py
@@ -182,18 +182,23 @@
         q1, r1 = lax.div(h, STEPS1), lax.rem(h, STEPS1)
         q0, r0 = lax.div(h, STEPS0), lax.rem(h, STEPS0)
 
-        def some(parity):
+        def some(alone, kind):
             todo = []
             for r in (2, 3, 4, 5, 0, 1, 6, 7, 8, 9, 10, 11, 12):
                 from1, from0 = STEPS1 - 1 + OFF1[r], START0 + STEPS0 - 1 + OFF0[r]
-                if from1 % 2 != parity:
+                if from1 % (STEPS1 if alone else 2) != kind:
                     continue
-                one = (r1 == from1 % STEPS1) & (h >= from1) & (h < from1 + STEPS1 * NS)
+                one = (h >= from1) & (h < from1 + STEPS1 * NS)
+                s = q1 - from1 // STEPS1
+                if alone:
+                    todo.append((r, s, one, one))
+                    continue
+                one = one & (r1 == from1 % STEPS1)
 
                 def zero(count):
                     return (r0 == from0 % STEPS0) & (h >= from0) & (h < from0 + STEPS0 * count)
 
-                s = jnp.where(h >= from0, NS + q0 - from0 // STEPS0, q1 - from1 // STEPS1)
+                s = jnp.where(h >= from0, NS + q0 - from0 // STEPS0, s)
                 prepared = one | zero(NS if r <= 6 else Q)
                 todo.append((r, s, prepared, one | zero(Q) if r == 6 else prepared))
             for r, s, prepared, _ in todo:
@@ -208,8 +213,17 @@
                     if r < NR:
                         start(r, s)
 
-        for parity in range(2):
-            pl.when(lax.rem(h, 2) == parity)(functools.partial(some, parity))
+        first = START0 + STEPS0 - 1
+
+        @pl.when(h < first)
+        def _():
+            for kind in range(STEPS1):
+                pl.when(r1 == kind)(functools.partial(some, True, kind))
+
+        @pl.when(h >= first)
+        def _():
+            for kind in range(2):
+                pl.when(lax.rem(h, 2) == kind)(functools.partial(some, False, kind))
 
     def weights(i):
         slot = lax.rem(i, 2)

time: 530 us -> 526 us (level)
  no operation moved by 1% of the time
where the time goes in v5:
time: 526 us
  Pallas kernels  504 us (96%)
  between operations  14.1 us (3%)
  waiting for transfers between devices  7.81 us (1%)
    pallas_call x1, Pallas kernels, gradients(): pl.pallas_call(step_kernel, name='gradients', in_specs=[anyspec] * 5, out...  351 us
    pallas_call x2, Pallas kernels, adam(): pl.pallas_call(functools.partial(adam_kernel, gathered), name='adamw_rest...  153 us
  transfers between devices with their start and end apart: 1, of which 1 were waited for; matrix products, arithmetic and copies ran while one was open for 0% of the time, Pallas kernels for 18%

profile of v5, /device:TPU:1, one launch (start us, length us, event | category | flops | bytes accessed | tf_op | source)
XLA Modules:
  0.0 526.1 jit_solution(6872374006243550838)
XLA Ops:
  7.2 0.0 all-gather.3.cloned.1.call-start
  7.2 351.4 %gradients.1 = (bf16[3,16,1024,256]{3,2,1,0:T(8,128)(2,1)}, bf16[3,10,16,256]{3,2,1,0:T(8,128)(2,1)}, f32[13,2048,256]{2,1,0:T(8,128)}, f32[13,2048,256]{2,1,0:T...) custom-call(bf16[2048,1024]{1,0:T(8,128)(2,1)} %bitcast.6, bf16[2048,1024]{1,0:T(8,128)(2,1)} %bitcast.7, ...), custom_call_target="tpu_custom_call" | custom-call | flops 209379655680 | bytes 250000000 | tf_op jit(solution)/shard_map/gradients/pallas_call | solution.py:526
  358.6 0.0 all-gather.3.cloned.1.call-update
  358.6 93.6 %adamw.1 = (bf16[2,1024,3328]{2,1,0:T(8,128)(2,1)}, bf16[2,1024,3328]{2,1,0:T(8,128)(2,1)}, bf16[2,3328,1024]{2,1,0:T(8,128)(2,1)}, f32[2,1024,3328]{2,1,0:T(8,1...) custom-call(bf16[2,1024,3328]{2,1,0:T(8,128)(2,1)} %refs_0_.3, ...), custom_call_target="tpu_custom_call" | custom-call | flops 10000000000 | bytes 276824064 | tf_op jit(solution)/shard_map/adamw/pallas_call | solution.py:629
  452.2 7.8 %all-gather.3.cloned.1.call-done = bf16[192,10,16,256]{3,2,1,0:T(8,128)(2,1)} async-done(((bf16[3,10,16,256]{3,2,1,0:T(8,128)(2,1)}), bf16[192,10,16,256]{3,2,1,0:T(8,128)(2,1)}) %all-gather.3.cloned.1.call-update) | async-done | bytes 15728656 | tf_op jit(solution)/shard_map/all_gather | solution.py:648
  460.0 59.2 %adamw_rest.1 = (bf16[2,1024,3328]{2,1,0:T(8,128)(2,1)}, bf16[2,1024,3328]{2,1,0:T(8,128)(2,1)}, bf16[2,3328,1024]{2,1,0:T(8,128)(2,1)}, f32[2,1024,3328]{2,1,0:...) custom-call(bf16[2,1024,3328]{2,1,0:T(8,128)(2,1)} %refs_0_.3, ...), custom_call_target="tpu_custom_call", output_to_operand_aliasing={{0}: (12, {}), {1}: (13, {}), {2}: (14, {}), {3}: (15, {}),... | custom-call | flops 10000000000 | bytes 173015040 | tf_op jit(solution)/shard_map/adamw_rest/pallas_call | solution.py:629
Async XLA Ops:
  7.2 452.9 %all-gather.3.cloned.1.call-start = ((), (), s32[]{:S(2)}) async-start(), calls=%async_computation | async-start | bytes 15974400 | tf_op jit(solution)/shard_map/all_gather | solution.py:648
Sparse Core Ops, SparseCore 0:
  358.8 101.2 all-gather.2
